TPU v7x, 128 devices: a whole 4x4x4 slice. The times are simulated.
128 devices in a mesh: dp: 128 (over y, x, z, core).
Axes of the slice: x: 4, y: 4, z: 4, core: 2. Of those that a mesh axis runs over, the one named last changes fastest.
Arguments:
- patches: bfloat16 [98304, 1280], P('dp'), may hold values from -6 to 6
- patch_grids: int32 [768, 4, 2], P('dp'), may hold values from 0 to 16, as said below
- block_counts: int32 [128], replicated, may hold values from 0 to 6, as said below
- send_counts: int32 [7, 128], replicated, may hold values from 0 to 2, as said below
- row_table: bfloat16 [16, 1280], replicated, may hold values from -3 to 3
- col_table: bfloat16 [16, 1280], replicated, may hold values from -3 to 3
- ln_gain: bfloat16 [1280], replicated, may hold values from 0.25 to 1.75
- ln_bias: bfloat16 [1280], replicated, may hold values from -3 to 3
- w_qkv: bfloat16 [1280, 1920], replicated, may hold values from -1.2 to 1.2
- b_qkv: bfloat16 [1920], replicated, may hold values from -3 to 3
- w_out: bfloat16 [640, 1280], replicated, may hold values from -0.25 to 0.25
- b_out: bfloat16 [1280], replicated, may hold values from -3 to 3
- cotangent: bfloat16 [65536, 1280], P('dp'), may hold values from -1.5 to 1.5
Outputs:
- block_output: bfloat16 [65536, 1280], P('dp')
- grad_w_qkv: float32 [1280, 1920], P('dp')
- grad_w_out: float32 [640, 1280], P('dp')
Inputs may be any that keep to these rules, and one draw needn't show every extreme that they name: `patch_grids`: in each block slot the areas h * w of its 4 images sum to at most 128; heights are 1 to 16, widths 0 to 16, width 0 meaning no image. `block_counts`: live blocks of each rank at the start; with send_counts no rank holds more than 6 live blocks during balancing, and after the last section every rank holds 2 to 4, some rank exactly 4. `send_counts`: A rank never sends more blocks than it holds live; of two partners in a section at most one sends; in every draw some rank sends exactly 2 blocks in the last section.
All inputs are finite; a program needn't handle non-finite values.
Results may differ from a plain program's by a relative error of at most 0.0075.
Values may be sent and summed in bfloat16 or wider, within the bound.
No kernel may reach another device: no remote copies, remote signals or barrier semaphores. Data moves between devices by JAX's collectives and lax.ppermute only.
A program may use at most 128 MiB of HBM per device.

v0:
```python
import math

import jax
import jax.numpy as jnp
from jax import lax
from jax.sharding import PartitionSpec as P

HEAD = 80
BLOCK = 128


EPSILON = 1e-06


def partner_2(value, axis, stride):
    return lax.ppermute(value, axis, [(i, i ^ 1 << stride) for i in range(lax.axis_size(axis))])


def token_layout(patch_grids):
    heights = patch_grids[:, :, 0]
    widths = patch_grids[:, :, 1]
    image_area = heights * widths
    image_end = jnp.cumsum(image_area, axis=1)
    image_start = image_end - image_area
    positions = jnp.arange(BLOCK, dtype=jnp.int32)[None, :, None]
    member = ((positions >= image_start[:, None, :]) & (positions < image_end[:, None, :])).astype(
        jnp.int32
    )
    image_ids = jnp.arange(patch_grids.shape[1], dtype=jnp.int32)
    in_image = jnp.sum(member, axis=-1)
    segment = jnp.sum(member * image_ids, axis=-1) + in_image - 1
    offset = positions[:, :, 0] - jnp.sum(member * image_start[:, None, :], axis=-1)
    offset = offset * in_image
    span = jnp.maximum(jnp.sum(member * widths[:, None, :], axis=-1), 1)
    row_index = offset // span
    col_index = offset - row_index * span
    return (segment, row_index, col_index, in_image)


def embed_blocks(patch_rows, patch_grids, row_table, col_table):
    block_total = patch_grids.shape[0]
    segment, row_index, col_index, in_image = token_layout(patch_grids)
    levels = jnp.arange(row_table.shape[0], dtype=jnp.int32)
    row_hot = (row_index.reshape(-1, 1) == levels[None, :]).astype(jnp.bfloat16)
    col_hot = (col_index.reshape(-1, 1) == levels[None, :]).astype(jnp.bfloat16)
    table_sum = jnp.dot(row_hot, row_table, preferred_element_type=jnp.float32) + jnp.dot(
        col_hot, col_table, preferred_element_type=jnp.float32
    )
    embedded = (
        patch_rows.astype(jnp.float32) + table_sum * in_image.reshape(-1, 1).astype(jnp.float32)
    ).astype(jnp.bfloat16)
    return (embedded.reshape(block_total, BLOCK, patch_rows.shape[1]), segment)


def layer_forward(blocks, marks, ln_gain, ln_bias, w_qkv, b_qkv, w_out, b_out):
    block_total = blocks.shape[0]
    model_width = blocks.shape[2]
    inner = w_out.shape[0]
    head_count = inner // HEAD
    rows = blocks.reshape(block_total * BLOCK, model_width).astype(jnp.float32)
    average = jnp.mean(rows, axis=-1, keepdims=True)
    centred = rows - average
    variance = jnp.mean(centred * centred, axis=-1, keepdims=True)
    normed = (
        centred * lax.rsqrt(variance + EPSILON) * ln_gain.astype(jnp.float32)
        + ln_bias.astype(jnp.float32)
    ).astype(jnp.bfloat16)
    mixed = (
        jnp.dot(normed, w_qkv, preferred_element_type=jnp.float32) + b_qkv.astype(jnp.float32)
    ).astype(jnp.bfloat16)
    shaped = mixed.reshape(block_total, BLOCK, 3, head_count, HEAD).astype(jnp.float32)
    query_f = shaped[:, :, 0]
    key_f = shaped[:, :, 1]
    value_f = shaped[:, :, 2]
    score_scale = 1.0 / math.sqrt(HEAD)
    scores = jnp.einsum("bqhd,bkhd->bhqk", query_f, key_f) * score_scale
    same_image = marks[:, :, None] == marks[:, None, :]
    scores = jnp.where(same_image[:, None], scores, -1e30)
    top_score = jnp.max(scores, axis=-1, keepdims=True)
    expo = jnp.exp(scores - top_score)
    probs_f = expo / jnp.sum(expo, axis=-1, keepdims=True)
    probs_b = probs_f.astype(jnp.bfloat16)
    attended = jnp.einsum("bhqk,bkhd->bqhd", probs_b.astype(jnp.float32), value_f)
    attended = attended.reshape(block_total * BLOCK, inner).astype(jnp.bfloat16)
    projected = jnp.dot(attended, w_out, preferred_element_type=jnp.float32) + b_out.astype(
        jnp.float32
    )
    result = (rows + projected).astype(jnp.bfloat16)
    return (result, (normed, query_f, key_f, value_f, probs_f, probs_b, attended))


def output_backward(out_grad, saved, w_out):
    normed, query_f, key_f, value_f, probs_f, probs_b, attended = saved
    grad_out = jnp.dot(attended.T, out_grad, preferred_element_type=jnp.float32)
    attn_grad = jnp.dot(out_grad, w_out.T, preferred_element_type=jnp.float32)
    return (grad_out, attn_grad.reshape(query_f.shape))


def qkv_backward(attn_grad, saved):
    normed, query_f, key_f, value_f, probs_f, probs_b, attended = saved
    score_scale = 1.0 / math.sqrt(HEAD)
    prob_grad = jnp.einsum("bqhd,bkhd->bhqk", attn_grad, value_f)
    value_grad = jnp.einsum("bhqk,bqhd->bkhd", probs_b.astype(jnp.float32), attn_grad)
    score_grad = (
        probs_f * (prob_grad - jnp.sum(prob_grad * probs_f, axis=-1, keepdims=True)) * score_scale
    )
    query_grad = jnp.einsum("bhqk,bkhd->bqhd", score_grad, key_f)
    key_grad = jnp.einsum("bhqk,bqhd->bkhd", score_grad, query_f)
    row_total = query_f.shape[0] * query_f.shape[1]
    mixed_grad = (
        jnp.stack([query_grad, key_grad, value_grad], axis=2)
        .reshape(row_total, -1)
        .astype(jnp.bfloat16)
    )
    return jnp.dot(normed.T, mixed_grad, preferred_element_type=jnp.float32)


def local(
    patches,
    patch_grids,
    block_counts,
    send_counts,
    row_table,
    col_table,
    ln_gain,
    ln_bias,
    w_qkv,
    b_qkv,
    w_out,
    b_out,
    cotangent,
):
    slot_count = patches.shape[0] // BLOCK
    balanced = cotangent.shape[0] // BLOCK
    spare_slots = slot_count - balanced
    embedded, segment = embed_blocks(patches, patch_grids, row_table, col_table)
    segment_marks = segment.astype(jnp.bfloat16)
    all_ranks = jnp.arange(block_counts.shape[0], dtype=jnp.int32)
    own_rank = lax.axis_index("dp")
    counts = block_counts
    slot_ids = jnp.arange(slot_count, dtype=jnp.int32)
    section_total = lax.axis_size("dp").bit_length() - 1
    for section_index in range(section_total):
        partner = jnp.bitwise_xor(all_ranks, 1 << section_index)
        sent_now = send_counts[section_index]
        received = sent_now[partner]
        own_count = counts[own_rank]
        leaving = sent_now[own_rank]
        arriving = received[own_rank]
        staying = slot_ids < own_count - leaving
        landing = (slot_ids >= own_count) & (slot_ids < own_count + arriving)
        picked = jnp.clip(
            own_count - leaving + jnp.arange(spare_slots, dtype=jnp.int32), 0, slot_count - 1
        )
        far_blocks, far_marks = partner_2(
            (jnp.take(embedded, picked, axis=0), jnp.take(segment_marks, picked, axis=0)),
            "dp",
            section_index,
        )
        source = jnp.clip(slot_ids - own_count, 0, spare_slots - 1)
        arrived = jnp.take(far_blocks, source, axis=0)
        arrived_marks = jnp.take(far_marks, source, axis=0)
        embedded = jnp.where(
            staying[:, None, None],
            embedded,
            jnp.where(landing[:, None, None], arrived, jnp.zeros_like(embedded)),
        )
        segment_marks = jnp.where(
            staying[:, None],
            segment_marks,
            jnp.where(landing[:, None], arrived_marks, -jnp.ones_like(segment_marks)),
        )
        counts = counts - sent_now + received
    live_count = counts[own_rank]
    rank_blocks = embedded[:balanced]
    rank_marks = segment_marks[:balanced]
    rank_live = jnp.arange(balanced, dtype=jnp.int32) < live_count
    result, saved = layer_forward(
        rank_blocks, rank_marks, ln_gain, ln_bias, w_qkv, b_qkv, w_out, b_out
    )
    slot_live = jnp.repeat(rank_live, BLOCK).reshape(-1, 1)
    result = jnp.where(slot_live, result, jnp.zeros_like(result))
    token_live = (rank_live[:, None] & (rank_marks >= 0)).reshape(-1, 1)
    out_grad = jnp.where(token_live, cotangent, jnp.zeros_like(cotangent))
    grad_out, attn_grad = output_backward(out_grad, saved, w_out)
    grad_qkv = qkv_backward(attn_grad, saved)
    qkv_rows, out_rows = (
        lax.psum_scatter(grad_qkv, "dp", scatter_dimension=0, tiled=True),
        lax.psum_scatter(grad_out, "dp", scatter_dimension=0, tiled=True),
    )
    return (result, qkv_rows, out_rows)


def solution(mesh):
    return jax.shard_map(
        local,
        mesh=mesh,
        in_specs=(
            P("dp", None),
            P("dp", None, None),
            P(),
            P(),
            P(),
            P(),
            P(),
            P(),
            P(),
            P(),
            P(),
            P(),
            P("dp", None),
        ),
        out_specs=(P("dp", None), P("dp", None), P("dp", None)),
        check_vma=False,
    )
```

profile of v0, /device:TPU:1, one launch (start us, length us, event | category | flops | bytes accessed | tf_op | source)
XLA Modules:
  0.0 444.0 jit_solution(8955730043745129842)
XLA Ops:
  69.2 3.7 fusion.19
  78.4 13.3 %collective-permute-done.8 = bf16[2,128]{1,0:T(2,128)(2,1)S(1)} collective-permute-done((bf16[2,128]{1,0:T(2,128)(2,1)S(1)}, bf16[2,128]{1,0:T(2,128)(2,1)S(1)}, u32[]{:S(2)}, u32[]{:S(2)}) %collective-permute-start.8) | collective-permute-done | bytes 544 | tf_op jit(solution)/shard_map/ppermute | solution.py:16
  94.3 3.7 fusion.18
  100.3 3.2 collective-permute-start.2
  104.3 12.9 %collective-permute-done.9 = bf16[2,128]{1,0:T(2,128)(2,1)S(1)} collective-permute-done((bf16[2,128]{1,0:T(2,128)(2,1)S(1)}, bf16[2,128]{1,0:T(2,128)(2,1)S(1)}, u32[]{:S(2)}, u32[]{:S(2)}) %collective-permute-start.9) | collective-permute-done | bytes 544 | tf_op jit(solution)/shard_map/ppermute | solution.py:16
  120.5 3.7 fusion.17
  128.1 12.7 %collective-permute-done.10 = bf16[2,128]{1,0:T(2,128)(2,1)S(1)} collective-permute-done((bf16[2,128]{1,0:T(2,128)(2,1)S(1)}, bf16[2,128]{1,0:T(2,128)(2,1)S(1)}, u32[]{:S(2)}, u32[]{:S(2)}) %collective-permute-start.10) | collective-permute-done | bytes 544 | tf_op jit(solution)/shard_map/ppermute | solution.py:16
  142.1 2.8 collective-permute-start.11
  146.9 3.7 fusion.16
  157.7 9.8 %collective-permute-done.4 = bf16[2,128,1280]{2,1,0:T(8,128)(2,1)S(1)} collective-permute-done((bf16[2,128,1280]{2,1,0:T(8,128)(2,1)S(1)}, bf16[2,128,1280]{2,1,0:T(8,128)(2,1)S(1)}, u32[]{:S(2)}, u32[]{:S(2)}) %collective-permute-start.4) | collective-permute-done | bytes 655392 | tf_op jit(solution)/shard_map/ppermute | solution.py:16
  169.5 3.7 fusion.15
  177.6 2.6 collective-permute-start.13
  181.0 8.9 %collective-permute-done.13 = bf16[2,128]{1,0:T(2,128)(2,1)S(1)} collective-permute-done((bf16[2,128]{1,0:T(2,128)(2,1)S(1)}, bf16[2,128]{1,0:T(2,128)(2,1)S(1)}, u32[]{:S(2)}, u32[]{:S(2)}) %collective-permute-start.13) | collective-permute-done | bytes 544 | tf_op jit(solution)/shard_map/ppermute | solution.py:16
  192.6 3.7 fusion.14
  199.1 3.3 fusion.44
  204.9 6.3 %collective-permute-done.6 = bf16[2,128,1280]{2,1,0:T(8,128)(2,1)S(1)} collective-permute-done((bf16[2,128,1280]{2,1,0:T(8,128)(2,1)S(1)}, bf16[2,128,1280]{2,1,0:T(8,128)(2,1)S(1)}, u32[]{:S(2)}, u32[]{:S(2)}) %collective-permute-start.6) | collective-permute-done | bytes 655392 | tf_op jit(solution)/shard_map/ppermute | solution.py:16
  216.7 6.5 %add_convert_fusion = bf16[512,1920]{1,0:T(8,128)(2,1)} fusion(bf16[512,1280]{1,0:T(8,128)(2,1)S(1)} %fusion.10, bf16[1280,1920]{1,0:T(8,128)(2,1)} %param.29, f32[1920]{0:T(1024)S(1)} %convert_element_type.98), kind=kOutput, calls=%fused_computation.39 | convolution fusion | flops 2518548480 | bytes 8199680 | tf_op jit(solution)/shard_map/dot_general | solution.py:69
  223.2 6.4 %reshape.839 = bf16[4,128,3,8,80]{4,3,2,1,0:T(8,128)(2,1)} reshape(bf16[512,1920]{1,0:T(8,128)(2,1)} %add_convert_fusion) | data formatting | bytes 3932160 | tf_op jit(solution)/shard_map/reshape | solution.py:71
  229.6 3.6 fusion.89
  240.2 3.5 fusion.92
  253.0 2.9 fusion.32
  255.9 5.3 %fusion.11 = f32[1280,1920]{1,0:T(8,128)} fusion(bf16[512,1280]{1,0:T(8,128)(2,1)S(1)} %bitcast.205, bf16[240,8,4,128]{3,2,1,0:T(4,128)(2,1)S(1)} %bitcast.204), kind=kOutput, calls=%fused_computation.57 | convolution fusion | flops 2516582400 | bytes 13107200 | tf_op jit(solution)/shard_map/dot_general | solution.py:115
  261.9 3.4 fusion.6
  265.4 168.7 %all-reduce.5.cloned.1.call-done = (f32[1280,1920]{1,0:T(8,128)}, f32[640,1280]{1,0:T(8,128)}) async-done(((f32[1280,1920]{1,0:T(8,128)}, f32[640,1280]{1,0:T(8,128)}), (f32[1280,1920]{1,0:T(8,128)}, f32[640,1280]{1,0:T(8,128)})) %all-reduce.5.cloned.1.call-update) | async-done | bytes 13107216
  (236 shorter events, 112.9 us)
Async XLA Ops:
  7.2 192.0 %copy-start = (bf16[640,1280]{1,0:T(8,128)(2,1)S(1)}, bf16[640,1280]{1,0:T(8,128)(2,1)}, u32[]{:S(2)}) copy-start(bf16[640,1280]{1,0:T(8,128)(2,1)} %param.31) | copy-start | bytes 4915204
  7.2 426.8 %all-reduce.5.cloned.1.call-start = ((), (), s32[]{:S(2)}) async-start(), calls=%async_computation | async-start | bytes 26214400
  13.2 63.8 %collective-permute-start.7 = (bf16[2,128]{1,0:T(2,128)(2,1)S(1)}, bf16[2,128]{1,0:T(2,128)(2,1)S(1)}, u32[]{:S(2)}, u32[]{:S(2)}) collective-permute-start(bf16[2,128]{1,0:T(2,128)(2,1)S(1)} %broadcast_select_fusion.16), channel_id=1, source_target_pairs={{0,1},{1,0},{2,3},{3,2},{4,5},{5,4},{6,7},{7,6},{8,9},{9,8},{10,11... | collective-permute-start | bytes 1544 | tf_op jit(solution)/shard_map/ppermute | solution.py:16
  21.0 10.8 %copy-start.9 = (s32[7,128]{1,0:T(8,128)S(1)}, s32[7,128]{1,0:T(8,128)}, u32[]{:S(2)}) copy-start(s32[7,128]{1,0:T(8,128)} %param.24) | copy-start | bytes 10756
  21.0 10.8 %copy-start.15 = (s32[128]{0:T(128)S(1)}, s32[128]{0:T(128)}, u32[]{:S(2)}) copy-start(s32[128]{0:T(128)} %param.23) | copy-start | bytes 1540
  21.0 46.2 %collective-permute-start = (bf16[2,128,1280]{2,1,0:T(8,128)(2,1)S(1)}, bf16[2,128,1280]{2,1,0:T(8,128)(2,1)S(1)}, u32[]{:S(2)}, u32[]{:S(2)}) collective-permute-start(bf16[2,128,1280]{2,1,0:T(8,128)(2,1)S(1)} %broadcast_select_fusion.7), channel_id=1, source_target_pairs={{0,1},{1,0},{2,3},{3,2},{4,5},{5,4},{6,7},{7,6},{8,9},{9,8},{10,11... | collective-permute-start | bytes 1966088 | tf_op jit(solution)/shard_map/ppermute | solution.py:16
  75.2 17.0 %collective-permute-start.1 = (bf16[2,128,1280]{2,1,0:T(8,128)(2,1)S(1)}, bf16[2,128,1280]{2,1,0:T(8,128)(2,1)S(1)}, u32[]{:S(2)}, u32[]{:S(2)}) collective-permute-start(bf16[2,128,1280]{2,1,0:T(8,128)(2,1)S(1)} %broadcast_select_fusion.6), channel_id=1, source_target_pairs={{0,2},{1,3},{2,0},{3,1},{4,6},{5,7},{6,4},{7,5},{8,10},{9,11},{10,... | collective-permute-start | bytes 1966088 | tf_op jit(solution)/shard_map/ppermute | solution.py:16
  78.3 13.4 %collective-permute-start.8 = (bf16[2,128]{1,0:T(2,128)(2,1)S(1)}, bf16[2,128]{1,0:T(2,128)(2,1)S(1)}, u32[]{:S(2)}, u32[]{:S(2)}) collective-permute-start(bf16[2,128]{1,0:T(2,128)(2,1)S(1)} %broadcast_select_fusion.15), channel_id=1, source_target_pairs={{0,2},{1,3},{2,0},{3,1},{4,6},{5,7},{6,4},{7,5},{8,10},{9,11},{10,... | collective-permute-start | bytes 1544 | tf_op jit(solution)/shard_map/ppermute | solution.py:16
  100.3 18.1 %collective-permute-start.2 = (bf16[2,128,1280]{2,1,0:T(8,128)(2,1)S(1)}, bf16[2,128,1280]{2,1,0:T(8,128)(2,1)S(1)}, u32[]{:S(2)}, u32[]{:S(2)}) collective-permute-start(bf16[2,128,1280]{2,1,0:T(8,128)(2,1)S(1)} %broadcast_select_fusion.5), channel_id=1, source_target_pairs={{0,4},{1,5},{2,6},{3,7},{4,0},{5,1},{6,2},{7,3},{8,12},{9,13},{10,... | collective-permute-start | bytes 1966088 | tf_op jit(solution)/shard_map/ppermute | solution.py:16
  104.2 13.0 %collective-permute-start.9 = (bf16[2,128]{1,0:T(2,128)(2,1)S(1)}, bf16[2,128]{1,0:T(2,128)(2,1)S(1)}, u32[]{:S(2)}, u32[]{:S(2)}) collective-permute-start(bf16[2,128]{1,0:T(2,128)(2,1)S(1)} %broadcast_select_fusion.14), channel_id=1, source_target_pairs={{0,4},{1,5},{2,6},{3,7},{4,0},{5,1},{6,2},{7,3},{8,12},{9,13},{10,... | collective-permute-start | bytes 1544 | tf_op jit(solution)/shard_map/ppermute | solution.py:16
  126.5 18.3 %collective-permute-start.3 = (bf16[2,128,1280]{2,1,0:T(8,128)(2,1)S(1)}, bf16[2,128,1280]{2,1,0:T(8,128)(2,1)S(1)}, u32[]{:S(2)}, u32[]{:S(2)}) collective-permute-start(bf16[2,128,1280]{2,1,0:T(8,128)(2,1)S(1)} %broadcast_select_fusion.4), channel_id=1, source_target_pairs={{0,8},{1,9},{2,10},{3,11},{4,12},{5,13},{6,14},{7,15},{8,0},{9,1},... | collective-permute-start | bytes 1966088 | tf_op jit(solution)/shard_map/ppermute | solution.py:16
  127.9 12.9 %collective-permute-start.10 = (bf16[2,128]{1,0:T(2,128)(2,1)S(1)}, bf16[2,128]{1,0:T(2,128)(2,1)S(1)}, u32[]{:S(2)}, u32[]{:S(2)}) collective-permute-start(bf16[2,128]{1,0:T(2,128)(2,1)S(1)} %broadcast_select_fusion.13), channel_id=1, source_target_pairs={{0,8},{1,9},{2,10},{3,11},{4,12},{5,13},{6,14},{7,15},{8,0},{9,1},... | collective-permute-start | bytes 1544 | tf_op jit(solution)/shard_map/ppermute | solution.py:16
  142.1 11.1 %collective-permute-start.11 = (bf16[2,128]{1,0:T(2,128)(2,1)S(1)}, bf16[2,128]{1,0:T(2,128)(2,1)S(1)}, u32[]{:S(2)}, u32[]{:S(2)}) collective-permute-start(bf16[2,128]{1,0:T(2,128)(2,1)S(1)} %broadcast_select_fusion.12), channel_id=1, source_target_pairs={{0,16},{1,17},{2,18},{3,19},{4,20},{5,21},{6,22},{7,23},{8,24},{9,... | collective-permute-start | bytes 1544 | tf_op jit(solution)/shard_map/ppermute | solution.py:16
  152.9 14.6 %collective-permute-start.4 = (bf16[2,128,1280]{2,1,0:T(8,128)(2,1)S(1)}, bf16[2,128,1280]{2,1,0:T(8,128)(2,1)S(1)}, u32[]{:S(2)}, u32[]{:S(2)}) collective-permute-start(bf16[2,128,1280]{2,1,0:T(8,128)(2,1)S(1)} %broadcast_select_fusion.3), channel_id=1, source_target_pairs={{0,16},{1,17},{2,18},{3,19},{4,20},{5,21},{6,22},{7,23},{8,24},{9,... | collective-permute-start | bytes 1966088 | tf_op jit(solution)/shard_map/ppermute | solution.py:16
  154.5 2.6 collective-permute-start.12
  173.2 7.7 %copy-start.11 = (bf16[1280]{0:T(1024)(128)(2,1)S(1)}, bf16[1280]{0:T(1024)(128)(2,1)}, u32[]{:S(2)}) copy-start(bf16[1280]{0:T(1024)(128)(2,1)} %param.28) | copy-start | bytes 7684
  173.2 7.7 %copy-start.12 = (bf16[1280]{0:T(1024)(128)(2,1)S(1)}, bf16[1280]{0:T(1024)(128)(2,1)}, u32[]{:S(2)}) copy-start(bf16[1280]{0:T(1024)(128)(2,1)} %param.27) | copy-start | bytes 7684
  173.2 7.7 %copy-start.13 = (bf16[1920]{0:T(1024)(128)(2,1)S(1)}, bf16[1920]{0:T(1024)(128)(2,1)}, u32[]{:S(2)}) copy-start(bf16[1920]{0:T(1024)(128)(2,1)} %param.30) | copy-start | bytes 11524
  175.6 15.0 %collective-permute-start.5 = (bf16[2,128,1280]{2,1,0:T(8,128)(2,1)S(1)}, bf16[2,128,1280]{2,1,0:T(8,128)(2,1)S(1)}, u32[]{:S(2)}, u32[]{:S(2)}) collective-permute-start(bf16[2,128,1280]{2,1,0:T(8,128)(2,1)S(1)} %broadcast_select_fusion.2), channel_id=1, source_target_pairs={{0,32},{1,33},{2,34},{3,35},{4,36},{5,37},{6,38},{7,39},{8,40},{9,... | collective-permute-start | bytes 1966088 | tf_op jit(solution)/shard_map/ppermute | solution.py:16
  177.6 12.3 %collective-permute-start.13 = (bf16[2,128]{1,0:T(2,128)(2,1)S(1)}, bf16[2,128]{1,0:T(2,128)(2,1)S(1)}, u32[]{:S(2)}, u32[]{:S(2)}) collective-permute-start(bf16[2,128]{1,0:T(2,128)(2,1)S(1)} %broadcast_select_fusion.10), channel_id=1, source_target_pairs={{0,64},{1,65},{2,66},{3,67},{4,68},{5,69},{6,70},{7,71},{8,72},{9,... | collective-permute-start | bytes 1544 | tf_op jit(solution)/shard_map/ppermute | solution.py:16
  190.6 8.6 %copy-start.10 = (bf16[6,128]{1,0:T(8,128)(2,1)}, bf16[6,128]{1,0:T(8,128)(2,1)S(1)}, u32[]{:S(2)}) copy-start(bf16[6,128]{1,0:T(8,128)(2,1)S(1)} %fusion.63) | copy-start | bytes 4612
  198.6 12.6 %collective-permute-start.6 = (bf16[2,128,1280]{2,1,0:T(8,128)(2,1)S(1)}, bf16[2,128,1280]{2,1,0:T(8,128)(2,1)S(1)}, u32[]{:S(2)}, u32[]{:S(2)}) collective-permute-start(bf16[2,128,1280]{2,1,0:T(8,128)(2,1)S(1)} %broadcast_select_fusion.1), channel_id=1, source_target_pairs={{0,64},{1,65},{2,66},{3,67},{4,68},{5,69},{6,70},{7,71},{8,72},{9,... | collective-permute-start | bytes 1966088 | tf_op jit(solution)/shard_map/ppermute | solution.py:16
  199.1 5.6 %slice-start = ((bf16[6,128]{1,0:T(8,128)(2,1)}), bf16[4,128]{1,0:T(4,128)(2,1)S(1)}, s32[]{:S(2)}) async-start(bf16[6,128]{1,0:T(8,128)(2,1)} %copy-done.10), calls=%async_computation.1 | async-start | bytes 2048 | tf_op jit(solution)/shard_map/slice | solution.py:176
  243.7 2.6 copy-start.16
  (9 other events, 13.6 us)
Sparse Core Ops, SparseCore 0:
  261.4 172.5 all-reduce.4
where the time goes:
time: 445 us; the launch traced here: 444 us
  waiting for transfers between devices  233 us (52%)
  local copies, waits for them, and re-layouts  88.1 us (20%)
  other arithmetic  38.9 us (9%)
  matrix products  34.1 us (8%)
  between operations  32.5 us (7%)
  starting transfers between devices  17.2 us (4%)
    unnamed x2, waiting for transfers between devices  169 us
    ppermute x14, waiting for transfers between devices, partner_2(): lax.ppermute(value, axis, [(i, i ^ 1 << stride) for i in range(lax.axis_s...  64.5 us
    select_n x6, other arithmetic, local(): jnp.where(staying[:, None, None], embedded, jnp.where(landing[:, None, No...  22.4 us
    ppermute x14, starting transfers between devices, partner_2(): lax.ppermute(value, axis, [(i, i ^ 1 << stride) for i in range(lax.axis_s...  17.2 us
    gather x7, local copies, waits for them, and re-layouts, local(): jnp.take(embedded, picked, axis=0)  15 us
    gather x7, local copies, waits for them, and re-layouts, local(): arrived = jnp.take(far_blocks, source, axis=0)  14.2 us
    unnamed x39, local copies, waits for them, and re-layouts  12 us
  transfers between devices with their start and end apart: 15, of which 8 were waited for; matrix products, arithmetic and copies ran while one was open for 16% of the time, Pallas kernels for 0%

commit v1 on v0

v1 whole, which is shorter than its diff:
```python
import functools
import math

import jax
import jax.numpy as jnp
from jax import lax
from jax.experimental import pallas as pl
from jax.experimental.pallas import tpu as pltpu
from jax.sharding import PartitionSpec as P

HEAD = 80
BLOCK = 128
EPSILON = 1e-06
AXIS = "dp"

MARK = 8
PIECES = (56, 72)
STACK = 8
WINDOW = 2
GROUPS = ((0,), (1, 2), (3, 4), (5, 6))
FIELDS = 8

SMEM = pl.BlockSpec(memory_space=pltpu.SMEM)
VMEM = pl.BlockSpec(memory_space=pltpu.VMEM)


def payload_rows(piece):
    return PIECES[piece] + (MARK if piece == 0 else 0)


def masks_of(group):
    first = 1 << GROUPS[group][0]
    if len(GROUPS[group]) == 1:
        return (first,)
    second = 1 << GROUPS[group][1]
    return (first, second, first ^ second)


def exchange(values, group):
    size = lax.axis_size(AXIS)
    return [
        lax.ppermute(value, AXIS, [(i, i ^ mask) for i in range(size)])
        for value, mask in zip(values, masks_of(group))
    ]


def plan_kernel(counts_ref, sends_ref, table_ref):
    me = lax.axis_index(AXIS)
    count = counts_ref[me]
    for group, sections in enumerate(GROUPS):
        first = 1 << sections[0]
        m_a = sends_ref[sections[0], me]
        n_a = sends_ref[sections[0], me ^ first]
        if len(sections) == 1:
            values = (count - m_a, 0, 0, count, n_a, count - m_a + n_a, 0, 0)
            after = count - m_a + n_a
        else:
            second = 1 << sections[1]
            m_b = sends_ref[sections[1], me]
            n_b = sends_ref[sections[1], me ^ second]
            passed_on = jnp.minimum(sends_ref[sections[1], me ^ first], m_a)
            forwarded = jnp.minimum(n_b, sends_ref[sections[0], me ^ first ^ second])
            floor = count - m_a + n_a - m_b
            values = (
                count - m_a,
                count - m_a - (m_b - jnp.minimum(m_b, n_a)),
                count - passed_on,
                count,
                jnp.clip(floor - count, 0, n_a),
                floor,
                n_b - forwarded,
                forwarded,
            )
            after = floor + n_b
        for field, value in enumerate(values):
            table_ref[group * FIELDS + field] = jnp.int32(value)
        count = after
    table_ref[len(GROUPS) * FIELDS] = count


def make_plan(block_counts, send_counts):
    return pl.pallas_call(
        plan_kernel,
        out_shape=jax.ShapeDtypeStruct((len(GROUPS) * FIELDS + 8,), jnp.int32),
        in_specs=[SMEM, SMEM],
        out_specs=SMEM,
        name="plan",
    )(block_counts, send_counts)


def cut(table_ref, stack_ref, window_refs, group):
    for which, window_ref in enumerate(window_refs):
        low = table_ref[group * FIELDS + which]
        for i in range(WINDOW):
            window_ref[i] = stack_ref[low + i]


def land(table_ref, stack_ref, far_refs, group):
    base = group * FIELDS
    floor = table_ref[base + 5]
    targets = (
        (table_ref[base + 3], table_ref[base + 4]),
        (floor, table_ref[base + 6]),
        (floor + table_ref[base + 6], table_ref[base + 7]),
    )
    for far_ref, (start, total) in zip(far_refs, targets):
        for i in range(WINDOW):

            @pl.when(i < total)
            def _():
                stack_ref[start + i] = far_ref[i]


def open_kernel(piece, begin, table_ref, patches_ref, *rest):
    if piece == 0:
        grids_ref, stack_ref, window_ref, sem = rest
    else:
        stack_ref, window_ref, sem = rest
    rows = PIECES[piece]
    slots = patches_ref.shape[0]
    copy = pltpu.make_async_copy(
        patches_ref.at[:, pl.ds(begin, rows)], stack_ref.at[pl.ds(0, slots), pl.ds(0, rows)], sem
    )
    copy.start()
    for slot in range(slots, STACK):
        stack_ref[slot] = jnp.zeros(stack_ref.shape[1:], stack_ref.dtype)
    if piece == 0:
        for slot in range(slots):
            stack_ref[slot, rows:, :] = grids_ref[slot]
    copy.wait()
    cut(table_ref, stack_ref, (window_ref,), 0)


def open_piece(table, patches, grids, piece):
    rows = payload_rows(piece)
    width = patches.shape[-1]
    begin = sum(PIECES[:piece])
    extra = (grids,) if piece == 0 else ()
    return pl.pallas_call(
        functools.partial(open_kernel, piece, begin),
        out_shape=(
            jax.ShapeDtypeStruct((STACK, rows, width), patches.dtype),
            jax.ShapeDtypeStruct((WINDOW, rows, width), patches.dtype),
        ),
        in_specs=[SMEM, pl.BlockSpec(memory_space=pl.ANY)] + [VMEM] * len(extra),
        out_specs=(VMEM, VMEM),
        scratch_shapes=[pltpu.SemaphoreType.DMA],
        name=f"open_{piece}",
    )(table, patches, *extra)


def turn_kernel(group, table_ref, old_ref, *rest):
    far_count = len(masks_of(group))
    fars = rest[:far_count]
    stack_ref = rest[far_count]
    windows = rest[far_count + 1 :]
    stack_ref[...] = old_ref[: stack_ref.shape[0]]
    land(table_ref, stack_ref, fars, group)
    if windows:
        cut(table_ref, stack_ref, windows, group + 1)


def turn(table, stack, fars, group, piece, balanced):
    last = group == len(GROUPS) - 1
    slots = balanced if last else STACK
    window = jax.ShapeDtypeStruct((WINDOW,) + stack.shape[1:], stack.dtype)
    sends = 0 if last else len(masks_of(group + 1))
    out = pl.pallas_call(
        functools.partial(turn_kernel, group),
        out_shape=(jax.ShapeDtypeStruct((slots,) + stack.shape[1:], stack.dtype),) + (window,) * sends,
        in_specs=[SMEM, VMEM] + [VMEM] * len(fars),
        out_specs=(VMEM,) * (1 + sends),
        name=f"turn_{group}_{piece}",
    )(table, stack, *fars)
    return out[0], list(out[1:])


def balance(patches, patch_grids, table, balanced):
    slots = patch_grids.shape[0]
    width = patches.shape[-1]
    blocks = patches.reshape(slots, BLOCK, width)
    grids = jnp.broadcast_to(
        jnp.pad(
            patch_grids.reshape(slots, 1, -1).astype(jnp.bfloat16),
            ((0, 0), (0, 0), (0, width - patch_grids[0].size)),
        ),
        (slots, MARK, width),
    )
    stacks, windows = [], []
    for piece in range(len(PIECES)):
        stack, window = open_piece(table, blocks, grids, piece)
        stacks.append(stack)
        windows.append([window])
    for group in range(len(GROUPS)):
        for piece in range(len(PIECES)):
            fars = exchange(windows[piece], group)
            stacks[piece], windows[piece] = turn(
                table, stacks[piece], fars, group, piece, balanced
            )
    return stacks


def dot_nt(a, b):
    return lax.dot_general(a, b, (((1,), (1,)), ((), ())), preferred_element_type=jnp.float32)


def dot_tn(a, b):
    return lax.dot_general(a, b, (((0,), (0,)), ((), ())), preferred_element_type=jnp.float32)


def dot_nn(a, b):
    return lax.dot_general(a, b, (((1,), (0,)), ((), ())), preferred_element_type=jnp.float32)


def image_of_tokens(grid, positions):
    images = grid.shape[1] // 2
    zero = jnp.zeros_like(positions)
    segment, first, span, inside = zero - 1.0, zero, zero + 1.0, zero
    start = jnp.zeros((1, 1), jnp.float32)
    for j in range(images):
        width = grid[:, 2 * j + 1 : 2 * j + 2]
        end = start + grid[:, 2 * j : 2 * j + 1] * width
        member = (positions >= start) & (positions < end)
        segment = jnp.where(member, float(j), segment)
        first = jnp.where(member, start, first)
        span = jnp.where(member, width, span)
        inside = jnp.where(member, 1.0, inside)
        start = end
    offset = (positions - first) * inside
    row = jnp.floor((offset + 0.5) / span)
    return segment, row, offset - row * span, inside


def layer_kernel(
    table_ref,
    *refs,
):
    pieces = len(PIECES)
    stack_refs = refs[:pieces]
    (
        levels_ref,
        gain_ref,
        bias_ref,
        wall_hbm,
        ball_ref,
        w_out_hbm,
        turn_out_ref,
        b_out_ref,
        cot_hbm,
        result_ref,
        given_ref,
        kept_ref,
        x_ref,
        normed_ref,
        mixed_ref,
        grad_ref,
        attended_ref,
        out_grad_ref,
        attn_grad_ref,
        lines_ref,
        seg_row_ref,
        seg_col_ref,
        wall_ref,
        w_out_ref,
        cot_ref,
        sems,
    ) = refs[pieces:]
    balanced = stack_refs[0].shape[0]
    width = x_ref.shape[1]
    tokens = balanced * BLOCK
    inner = w_out_ref.shape[0]
    heads = inner // HEAD
    live_count = table_ref[len(GROUPS) * FIELDS]
    images = 4
    copies = [
        pltpu.make_async_copy(src, dst, sems.at[i])
        for i, (src, dst) in enumerate(
            ((cot_hbm, cot_ref), (w_out_hbm, w_out_ref), (wall_hbm, wall_ref))
        )
    ]
    for copy in copies:
        copy.start()

    col = lax.broadcasted_iota(jnp.int32, (BLOCK, 1), 0).astype(jnp.float32)
    lane = lax.broadcasted_iota(jnp.int32, (1, BLOCK), 1).astype(jnp.float32)
    level = lax.broadcasted_iota(jnp.int32, (BLOCK, levels_ref.shape[0]), 1).astype(jnp.float32)
    half = float(levels_ref.shape[0] // 2)

    for slot in range(balanced):
        at = slot * BLOCK
        grid = stack_refs[0][slot, PIECES[0] : PIECES[0] + MARK, :BLOCK].astype(jnp.float32)
        grid = grid[0:1, : 2 * images]
        segment, row, column, inside = image_of_tokens(grid, col)
        seg_col_ref[at : at + BLOCK, :] = segment
        seg_row_ref[slot] = jnp.broadcast_to(
            image_of_tokens(grid, lane)[0], (8, BLOCK)
        )
        hot = jnp.where((level == row) | (level == column + half), inside, 0.0)
        emb = dot_nn(hot.astype(jnp.bfloat16), levels_ref[...])
        begin = 0
        for piece, rows in enumerate(PIECES):
            raw = stack_refs[piece][slot, :rows, :].astype(jnp.float32)
            x_ref[at + begin : at + begin + rows, :] = (
                raw + emb[begin : begin + rows, :]
            ).astype(jnp.bfloat16)
            begin += rows
        rows = x_ref[at : at + BLOCK, :].astype(jnp.float32)
        centred = rows - jnp.sum(rows, axis=1, keepdims=True) * (1.0 / width)
        variance = jnp.sum(centred * centred, axis=1, keepdims=True) * (1.0 / width)
        normed_ref[at : at + BLOCK, :] = (
            centred * lax.rsqrt(variance + EPSILON) * gain_ref[...] + bias_ref[...]
        ).astype(jnp.bfloat16)

    copies[0].wait()
    for slot in range(balanced):
        at = slot * BLOCK
        keep = (seg_col_ref[at : at + BLOCK, :] >= 0.0) & (slot < live_count)
        out_grad_ref[at : at + BLOCK, :] = jnp.where(
            keep, cot_ref[at : at + BLOCK, :].astype(jnp.float32), 0.0
        ).astype(jnp.bfloat16)
    copies[1].wait()
    attn_grad_ref[...] = dot_nt(w_out_ref[...], out_grad_ref[...]).astype(jnp.bfloat16)
    copies[2].wait()
    step = 640
    for at in range(0, wall_ref.shape[0], step):
        mixed_ref[at : at + step, :] = (
            dot_nt(wall_ref[at : at + step, :], normed_ref[...]) + ball_ref[at : at + step, :]
        ).astype(jnp.bfloat16)

    scale = 1.0 / math.sqrt(HEAD)

    def one_slot(slot, carry):
        at = pl.multiple_of(slot * BLOCK, BLOCK)
        span = pl.ds(at, BLOCK)
        same = seg_col_ref[span, :] == seg_row_ref[slot, 0:1, :]
        for head in range(heads):
            h = head * HEAD
            query = mixed_ref[h : h + HEAD, span]
            key = mixed_ref[inner + h : inner + h + HEAD, span]
            value = mixed_ref[2 * inner + h : 2 * inner + h + HEAD, span]
            attn_grad = attn_grad_ref[h : h + HEAD, span]
            scores = jnp.where(same, dot_tn(key, query) * scale, -1e30)
            expo = jnp.exp(scores - jnp.max(scores, axis=0, keepdims=True))
            probs = expo * (1.0 / jnp.sum(expo, axis=0, keepdims=True))
            probs_b = probs.astype(jnp.bfloat16)
            attended_ref[h : h + HEAD, span] = dot_nn(value, probs_b).astype(jnp.bfloat16)
            prob_grad = dot_tn(value, attn_grad)
            grad_ref[2 * inner + h : 2 * inner + h + HEAD, span] = dot_nt(
                attn_grad, probs_b
            ).astype(jnp.bfloat16)
            mean = jnp.sum(prob_grad * probs, axis=0, keepdims=True)
            score_grad = (probs * (prob_grad - mean) * scale).astype(jnp.bfloat16)
            grad_ref[h : h + HEAD, span] = dot_nn(key, score_grad).astype(jnp.bfloat16)
            grad_ref[inner + h : inner + h + HEAD, span] = dot_nt(query, score_grad).astype(
                jnp.bfloat16
            )
        return carry

    lax.fori_loop(0, balanced, one_slot, 0)

    for slot in range(balanced):
        at = slot * BLOCK
        projected = dot_tn(attended_ref[:, at : at + BLOCK], w_out_ref[...]) + b_out_ref[...]
        total = x_ref[at : at + BLOCK, :].astype(jnp.float32) + projected
        result_ref[at : at + BLOCK, :] = jnp.where(slot < live_count, total, 0.0).astype(
            jnp.bfloat16
        )

    turned = dot_nn(turn_out_ref[...], attended_ref[...]).astype(jnp.bfloat16)
    chips = given_ref.shape[0]
    qkv_tiles = 3 * inner // 128
    out_tiles = width // 128
    per_rank = width // (2 * chips)
    out_rank = inner // (2 * chips)
    base = 3 * inner
    even = 8 * chips
    for part, target in enumerate((given_ref, kept_ref)):
        row = base + part * per_rank * chips
        eights = mixed_ref[row : row + even, :]
        others = mixed_ref[row + even : row + per_rank * chips, :]
        rest = per_rank - 8
        group = 3
        for tile in range(0, qkv_tiles, group):
            piece = grad_ref[tile * 128 : (tile + group) * 128, :]
            block = dot_nt(eights, piece).astype(jnp.bfloat16)
            side = dot_nt(others, piece)
            for t in range(group):
                target[:, 8 * (tile + t) : 8 * (tile + t) + 8, :] = block[
                    :, t * 128 : (t + 1) * 128
                ].reshape(chips, 8, 128)
                for e in range(rest):
                    line = ((tile + t) * rest + e) * chips
                    lines_ref[line : line + chips, :] = side[
                        e * chips : (e + 1) * chips, t * 128 : (t + 1) * 128
                    ]
        block = dot_nn(turned[part * out_rank * chips : (part + 1) * out_rank * chips, :], out_grad_ref[...])
        for t in range(out_tiles):
            for e in range(out_rank):
                line = (qkv_tiles * rest + t * out_rank + e) * chips
                lines_ref[line : line + chips, :] = block[
                    e * chips : (e + 1) * chips, t * 128 : (t + 1) * 128
                ]
        count = qkv_tiles * rest + out_tiles * out_rank

        def one_chip(chip, carry):
            for b in range(count // 8):
                lines = lines_ref[pl.ds(chip + b * 8 * chips, 8, stride=chips), :]
                target[chip, 8 * qkv_tiles + 8 * b : 8 * qkv_tiles + 8 * b + 8, :] = lines.astype(
                    jnp.bfloat16
                )
            return carry

        lax.fori_loop(0, chips, one_chip, 0)


def layer(table, stacks, levels, gain, bias, wall, ball, w_out, turn_out, b_out, cotangent):
    width = cotangent.shape[1]
    tokens = cotangent.shape[0]
    balanced = tokens // BLOCK
    inner = w_out.shape[0]
    chips = lax.axis_size(AXIS) // 2
    lines = (width // (2 * chips) * 3 * inner + inner // (2 * chips) * width) // 128
    any_space = pl.BlockSpec(memory_space=pl.ANY)
    first = [VMEM] * len(stacks)
    bf16, f32 = jnp.bfloat16, jnp.float32
    return pl.pallas_call(
        layer_kernel,
        out_shape=(
            jax.ShapeDtypeStruct((tokens, width), bf16),
            jax.ShapeDtypeStruct((chips, lines, 128), bf16),
            jax.ShapeDtypeStruct((chips, lines, 128), bf16),
        ),
        in_specs=[SMEM]
        + first
        + [VMEM, VMEM, VMEM, any_space, VMEM, any_space, VMEM, VMEM, any_space],
        out_specs=(VMEM, VMEM, VMEM),
        scratch_shapes=[
            pltpu.VMEM((tokens, width), bf16),
            pltpu.VMEM((tokens, width), bf16),
            pltpu.VMEM((wall.shape[0], tokens), bf16),
            pltpu.VMEM((3 * inner, tokens), bf16),
            pltpu.VMEM((inner, tokens), bf16),
            pltpu.VMEM((tokens, width), bf16),
            pltpu.VMEM((inner, tokens), bf16),
            pltpu.VMEM(((lines - 8 * (3 * inner // 128)) * chips, 128), f32),
            pltpu.VMEM((balanced, 8, BLOCK), f32),
            pltpu.VMEM((tokens, 1), f32),
            pltpu.VMEM(wall.shape, bf16),
            pltpu.VMEM(w_out.shape, bf16),
            pltpu.VMEM(cotangent.shape, bf16),
            pltpu.SemaphoreType.DMA((3,)),
        ],
        compiler_params=pltpu.CompilerParams(vmem_limit_bytes=60 * 1024 * 1024),
        name="layer",
    )(table, *stacks, levels, gain, bias, wall, ball, w_out, turn_out, b_out, cotangent)


def row_orders(width, inner):
    size = lax.axis_size(AXIS)
    chips = size // 2
    core = lax.axis_index(AXIS) & 1
    cores = jnp.stack([1 - core, core]).astype(jnp.int32)
    chip = jnp.arange(chips, dtype=jnp.int32)
    per, out = width // size, inner // size
    owner = (2 * chip[None, :] + cores[:, None]) * per
    eights = (owner[:, :, None] + jnp.arange(8, dtype=jnp.int32)).reshape(2, -1)
    others = (owner[:, None, :] + jnp.arange(8, per, dtype=jnp.int32)[None, :, None]).reshape(2, -1)
    qkv = jnp.concatenate([eights, others], axis=1).reshape(-1)
    owner = (2 * chip[None, :] + cores[:, None]) * out
    outs = (owner[:, None, :] + jnp.arange(out, dtype=jnp.int32)[None, :, None]).reshape(-1)
    return qkv, outs


def hot_rows(order):
    size = order.shape[0]
    return (order[:, None] == jnp.arange(size, dtype=jnp.int32)[None, :]).astype(jnp.bfloat16)


def chips_with_my_core(size):
    return [[2 * chip + core for chip in range(size // 2)] for core in range(2)]


def spread(given, kept, width, inner):
    size = lax.axis_size(AXIS)
    taken = lax.ppermute(given, AXIS, [(i, i ^ 1) for i in range(size)])
    pair = (kept.astype(jnp.float32) + taken.astype(jnp.float32)).astype(jnp.bfloat16)
    parts = lax.all_to_all(
        pair, AXIS, 0, 0, axis_index_groups=chips_with_my_core(size), tiled=True
    )
    total = jnp.sum(parts.astype(jnp.float32), axis=0)
    tiles, rest, out = 3 * inner // 128, width // size - 8, inner // size
    cuts = (8 * tiles, (8 + rest) * tiles)
    eights = total[: cuts[0]].reshape(tiles, 8, 128).transpose(1, 0, 2).reshape(8, -1)
    others = total[cuts[0] : cuts[1]].reshape(tiles, rest, 128).transpose(1, 0, 2).reshape(rest, -1)
    outs = total[cuts[1] :].reshape(width // 128, out, 128).transpose(1, 0, 2).reshape(out, -1)
    return jnp.concatenate([eights, others], axis=0), outs


def local(
    patches,
    patch_grids,
    block_counts,
    send_counts,
    row_table,
    col_table,
    ln_gain,
    ln_bias,
    w_qkv,
    b_qkv,
    w_out,
    b_out,
    cotangent,
):
    width, inner = cotangent.shape[1], w_out.shape[0]
    table = make_plan(block_counts, send_counts)
    qkv_order, out_order = row_orders(width, inner)
    wall = jnp.concatenate([w_qkv.T, hot_rows(qkv_order)], axis=0)
    ball = jnp.pad(b_qkv.astype(jnp.float32), (0, width)).reshape(-1, 1)
    stacks = balance(patches, patch_grids, table, cotangent.shape[0] // BLOCK)
    result, given, kept = layer(
        table,
        stacks,
        jnp.concatenate([row_table, col_table], axis=0),
        ln_gain.astype(jnp.float32).reshape(1, -1),
        ln_bias.astype(jnp.float32).reshape(1, -1),
        wall,
        ball,
        w_out,
        hot_rows(out_order),
        b_out.astype(jnp.float32).reshape(1, -1),
        cotangent,
    )
    qkv_rows, out_rows = spread(given, kept, width, inner)
    return (result, qkv_rows, out_rows)


def solution(mesh):
    return jax.shard_map(
        local,
        mesh=mesh,
        in_specs=(
            P("dp", None),
            P("dp", None, None),
            P(),
            P(),
            P(),
            P(),
            P(),
            P(),
            P(),
            P(),
            P(),
            P(),
            P("dp", None),
        ),
        out_specs=(P("dp", None), P("dp", None), P("dp", None)),
        check_vma=False,
    )
```

time: 445 us -> 228 us (0.51)
  waiting for transfers between devices: 233 us -> 53.8 us
  local copies, waits for them, and re-layouts: 88.1 us -> 17.1 us
  Pallas kernels: 0 us -> 67.8 us
  blocking collectives: 0 us -> 45.2 us
  matrix products: 34.1 us -> 0 us
  between operations: 32.5 us -> 0.84 us
  other arithmetic: 38.9 us -> 13.3 us
  starting transfers between devices: 17.2 us -> 28.7 us
    unnamed x2 -> x0, waiting for transfers between devices: 169 us -> none
    pallas_call x0 -> x12, Pallas kernels: none -> 67.8 us  [the longest x1 36.1 us: layer(): pl.pallas_call(layer_kernel, out_shape=(jax.ShapeDtypeStruct((tokens, wid...]
    gather x35 -> x0, local copies, waits for them, and re-layouts: 45.7 us -> none  [the longest x7 15 us: local(): jnp.take(embedded, picked, axis=0)]
    all_to_all x0 -> x1, blocking collectives: none -> 45.2 us  [spread(): lax.all_to_all(pair, AXIS, 0, 0, axis_index_groups=chips_with_my_core(siz...]
    dot_general x12 -> x0, matrix products: 30.6 us -> none  [the longest x1 6.49 us: layer_forward(): jnp.dot(normed, w_qkv, preferred_element_type=jnp.float32)]
    select_n x48 -> x0, other arithmetic: 28.9 us -> none  [the longest x6 22.4 us: local(): jnp.where(staying[:, None, None], embedded, jnp.where(landing[:, None, No...]
    dynamic_slice x22 -> x0, local copies, waits for them, and re-layouts: 14.1 us -> none  [the longest x7 4.87 us: local(): own_count = counts[own_rank]]
    ppermute x14 -> x21, starting transfers between devices: 17.2 us -> 28.7 us  [the longest x20 26.7 us: exchange(): lax.ppermute(value, AXIS, [(i, i ^ mask) for i in range(size)])]
  transfers between devices with their start and end apart: 15 -> 21, of which waited for: 8 -> 8; matrix products, arithmetic and copies ran while one was open for 16% -> 10% of each run, Pallas kernels for 0% -> 11%
where the time goes in v1:
time: 228 us; the launch traced here: 227 us
  Pallas kernels  67.8 us (30%)
  waiting for transfers between devices  53.8 us (24%)
  blocking collectives  45.2 us (20%)
  starting transfers between devices  28.7 us (13%)
  local copies, waits for them, and re-layouts  17.1 us (8%)
  other arithmetic  13.3 us (6%)
    ppermute x20, waiting for transfers between devices, exchange(): lax.ppermute(value, AXIS, [(i, i ^ mask) for i in range(size)])  48.2 us
    all_to_all x1, blocking collectives, spread(): lax.all_to_all(pair, AXIS, 0, 0, axis_index_groups=chips_with_my_core(siz...  45.2 us
    pallas_call x1, Pallas kernels, layer(): pl.pallas_call(layer_kernel, out_shape=(jax.ShapeDtypeStruct((tokens, wid...  36.1 us
    ppermute x20, starting transfers between devices, exchange(): lax.ppermute(value, AXIS, [(i, i ^ mask) for i in range(size)])  26.7 us
    pallas_call x8, Pallas kernels, turn(): pl.pallas_call(functools.partial(turn_kernel, group), out_shape=(jax.Shap...  24 us
    unnamed x35, local copies, waits for them, and re-layouts  11.5 us
    pallas_call x2, Pallas kernels, open_piece(): pl.pallas_call(functools.partial(open_kernel, piece, begin), out_shape=(j...  6.4 us
    concatenate x1, other arithmetic, local(): wall = jnp.concatenate([w_qkv.T, hot_rows(qkv_order)], axis=0)  6.14 us
  transfers between devices with their start and end apart: 21, of which 8 were waited for; matrix products, arithmetic and copies ran while one was open for 10% of the time, Pallas kernels for 11%

profile of v1, /device:TPU:1, one launch (start us, length us, event | category | flops | bytes accessed | tf_op | source)
XLA Modules:
  0.0 226.7 jit_solution(7025626587582350177)
XLA Ops:
  1.9 3.2 %open_1.1 = (bf16[8,72,1280]{2,1,0:T(8,128)(2,1)}, bf16[2,72,1280]{2,1,0:T(8,128)(2,1)}) custom-call(s32[40]{0:T(128)} %plan.1.table_ref, bf16[6,128,1280]{2,1,0:T(8,128)(2,1)} %bitcast.20), custom_call_target="tpu_custom_call" | custom-call | tf_op jit(solution)/shard_map/open_1/pallas_call | solution.py:139
  8.1 3.2 %open_0.1 = (bf16[8,64,1280]{2,1,0:T(8,128)(2,1)}, bf16[2,64,1280]{2,1,0:T(8,128)(2,1)}) custom-call(s32[40]{0:T(128)} %plan.1.table_ref, bf16[6,128,1280]{2,1,0:T(8,128)(2,1)} %bitcast.21, bf16[6,8,1280]{2,1,0:T(8,128)(2,1)} %broadcast_in_dim.5.rest_0_), custom_call_target="tpu_custom_call" | custom-call | tf_op jit(solution)/shard_map/open_0/pallas_call | solution.py:139
  14.0 2.9 %turn_0_0.1 = (bf16[8,64,1280]{2,1,0:T(8,128)(2,1)}, bf16[2,64,1280]{2,1,0:T(8,128)(2,1)}, bf16[2,64,1280]{2,1,0:T(8,128)(2,1)}, bf16[2,64,1280]{2,1,0:T(8,128)(2,1)}) custom-call(s32[40]{0:T(128)} %plan.1.table_ref, bf16[8,64,1280]{2,1,0:T(8,128)(2,1)} %get-tuple-element.34.old_ref, bf16[2,64,1280]{2,1,0:T(8,128)(2,1)} %copy-done.10), custom_call_target="tpu_custom_call" | custom-call | tf_op jit(solution)/shard_map/turn_0_0/pallas_call | solution.py:168
  18.6 3.3 %collective-permute-start.2 = (bf16[2,64,1280]{2,1,0:T(8,128)(2,1)}, bf16[2,64,1280]{2,1,0:T(8,128)(2,1)S(1)}, u32[]{:S(2)}, u32[]{:S(2)}) collective-permute-start(bf16[2,64,1280]{2,1,0:T(8,128)(2,1)} %get-tuple-element.38), channel_id=1, source_target_pairs={{0,4},{1,5},{2,6},{3,7},{4,0},{5,1},{6,2},{7,3},{8,12},{9,13},{10,... | collective-permute-start | bytes 983048 | tf_op jit(solution)/shard_map/ppermute | solution.py:42
  22.7 3.0 %turn_0_1.1 = (bf16[8,72,1280]{2,1,0:T(8,128)(2,1)}, bf16[2,72,1280]{2,1,0:T(8,128)(2,1)}, bf16[2,72,1280]{2,1,0:T(8,128)(2,1)}, bf16[2,72,1280]{2,1,0:T(8,128)(2,1)}) custom-call(s32[40]{0:T(128)} %plan.1.table_ref, bf16[8,72,1280]{2,1,0:T(8,128)(2,1)} %get-tuple-element.48.old_ref, bf16[2,72,1280]{2,1,0:T(8,128)(2,1)} %copy-done), custom_call_target="tpu_custom_call" | custom-call | tf_op jit(solution)/shard_map/turn_0_1/pallas_call | solution.py:168
  25.8 3.9 %collective-permute-start.12 = (bf16[2,72,1280]{2,1,0:T(8,128)(2,1)}, bf16[2,72,1280]{2,1,0:T(8,128)(2,1)}, u32[]{:S(2)}, u32[]{:S(2)}) collective-permute-start(bf16[2,72,1280]{2,1,0:T(8,128)(2,1)} %get-tuple-element.52), channel_id=1, source_target_pairs={{0,4},{1,5},{2,6},{3,7},{4,0},{5,1},{6,2},{7,3},{8,12},{9,13},{10,... | collective-permute-start | bytes 1105928 | tf_op jit(solution)/shard_map/ppermute | solution.py:42
  30.1 6.8 %collective-permute-done.2.rest_1_ = bf16[2,64,1280]{2,1,0:T(8,128)(2,1)S(1)} collective-permute-done((bf16[2,64,1280]{2,1,0:T(8,128)(2,1)}, bf16[2,64,1280]{2,1,0:T(8,128)(2,1)S(1)}, u32[]{:S(2)}, u32[]{:S(2)}) %collective-permute-start.2) | collective-permute-done | bytes 327712 | tf_op jit(solution)/shard_map/ppermute | solution.py:42
  39.7 3.1 %turn_1_0.1 = (bf16[8,64,1280]{2,1,0:T(8,128)(2,1)}, bf16[2,64,1280]{2,1,0:T(8,128)(2,1)}, bf16[2,64,1280]{2,1,0:T(8,128)(2,1)}, bf16[2,64,1280]{2,1,0:T(8,128)(2,1)}) custom-call(s32[40]{0:T(128)} %plan.1.table_ref, bf16[8,64,1280]{2,1,0:T(8,128)(2,1)} %get-tuple-element.36.old_ref, bf16[2,64,1280]{2,1,0:T(8,128)(2,1)} %copy-done.5, ...), custom_call_target="tpu_custom_call" | custom-call | tf_op jit(solution)/shard_map/turn_1_0/pallas_call | solution.py:168
  44.6 7.6 %copy.19 = bf16[1280,1920]{0,1:T(8,128)(2,1)} copy(bf16[1280,1920]{1,0:T(8,128)(2,1)} %param.21) | data formatting | bytes 9830400 | tf_op args[8]
  54.9 3.3 %turn_1_1.1 = (bf16[8,72,1280]{2,1,0:T(8,128)(2,1)}, bf16[2,72,1280]{2,1,0:T(8,128)(2,1)}, bf16[2,72,1280]{2,1,0:T(8,128)(2,1)}, bf16[2,72,1280]{2,1,0:T(8,128)(2,1)}) custom-call(s32[40]{0:T(128)} %plan.1.table_ref, bf16[8,72,1280]{2,1,0:T(8,128)(2,1)} %get-tuple-element.50.old_ref, bf16[2,72,1280]{2,1,0:T(8,128)(2,1)} %collective-permute-done.11.rest_0_, ...), custom_call_target="tpu_custom_call" | custom-call | tf_op jit(solution)/shard_map/turn_1_1/pallas_call | solution.py:168
  62.0 6.1 %pad_maximum_fusion.refs_5_ = bf16[3200,1280]{1,0:T(8,128)(2,1)} fusion(bf16[1280,1280]{1,0:T(8,128)(2,1)S(1)} %fusion, bf16[1920,1280]{1,0:T(8,128)(2,1)} %bitcast.19), kind=kLoop, calls=%fused_computation | loop fusion | flops 16384000 | bytes 16384000 | tf_op jit(solution)/shard_map/concatenate | solution.py:517
  68.2 5.0 %collective-permute-done.6.rest_2_ = bf16[2,64,1280]{2,1,0:T(8,128)(2,1)} collective-permute-done((bf16[2,64,1280]{2,1,0:T(8,128)(2,1)}, bf16[2,64,1280]{2,1,0:T(8,128)(2,1)}, u32[]{:S(2)}, u32[]{:S(2)}) %collective-permute-start.6) | collective-permute-done | bytes 327712 | tf_op jit(solution)/shard_map/ppermute | solution.py:42
  73.2 3.1 %turn_2_0.1 = (bf16[8,64,1280]{2,1,0:T(8,128)(2,1)}, bf16[2,64,1280]{2,1,0:T(8,128)(2,1)}, bf16[2,64,1280]{2,1,0:T(8,128)(2,1)}, bf16[2,64,1280]{2,1,0:T(8,128)(2,1)}) custom-call(s32[40]{0:T(128)} %plan.1.table_ref, bf16[8,64,1280]{2,1,0:T(8,128)(2,1)} %get-tuple-element.40.old_ref, bf16[2,64,1280]{2,1,0:T(8,128)(2,1)} %collective-permute-done.4.rest_0_, ...), custom_call_target="tpu_custom_call" | custom-call | tf_op jit(solution)/shard_map/turn_2_0/pallas_call | solution.py:168
  78.3 8.2 %collective-permute-done.16.rest_2_ = bf16[2,72,1280]{2,1,0:T(8,128)(2,1)} collective-permute-done((bf16[2,72,1280]{2,1,0:T(8,128)(2,1)}, bf16[2,72,1280]{2,1,0:T(8,128)(2,1)}, u32[]{:S(2)}, u32[]{:S(2)}) %collective-permute-start.16) | collective-permute-done | bytes 368672 | tf_op jit(solution)/shard_map/ppermute | solution.py:42
  86.4 3.3 %turn_2_1.1 = (bf16[8,72,1280]{2,1,0:T(8,128)(2,1)}, bf16[2,72,1280]{2,1,0:T(8,128)(2,1)}, bf16[2,72,1280]{2,1,0:T(8,128)(2,1)}, bf16[2,72,1280]{2,1,0:T(8,128)(2,1)}) custom-call(s32[40]{0:T(128)} %plan.1.table_ref, bf16[8,72,1280]{2,1,0:T(8,128)(2,1)} %get-tuple-element.54.old_ref, bf16[2,72,1280]{2,1,0:T(8,128)(2,1)} %collective-permute-done.14.rest_0_, ...), custom_call_target="tpu_custom_call" | custom-call | tf_op jit(solution)/shard_map/turn_2_1/pallas_call | solution.py:168
  91.0 2.6 %collective-permute-start.18 = (bf16[2,72,1280]{2,1,0:T(8,128)(2,1)}, bf16[2,72,1280]{2,1,0:T(8,128)(2,1)S(1)}, u32[]{:S(2)}, u32[]{:S(2)}) collective-permute-start(bf16[2,72,1280]{2,1,0:T(8,128)(2,1)} %get-tuple-element.60), channel_id=1, source_target_pairs={{0,64},{1,65},{2,66},{3,67},{4,68},{5,69},{6,70},{7,71},{8,72},{9,... | collective-permute-start | bytes 1105928 | tf_op jit(solution)/shard_map/ppermute | solution.py:42
  101.1 15.9 %collective-permute-done.8.rest_1_ = bf16[2,64,1280]{2,1,0:T(8,128)(2,1)S(1)} collective-permute-done((bf16[2,64,1280]{2,1,0:T(8,128)(2,1)}, bf16[2,64,1280]{2,1,0:T(8,128)(2,1)S(1)}, u32[]{:S(2)}, u32[]{:S(2)}) %collective-permute-start.8) | collective-permute-done | bytes 327712 | tf_op jit(solution)/shard_map/ppermute | solution.py:42
  117.0 9.1 %collective-permute-done.9.rest_2_ = bf16[2,64,1280]{2,1,0:T(8,128)(2,1)S(1)} collective-permute-done((bf16[2,64,1280]{2,1,0:T(8,128)(2,1)}, bf16[2,64,1280]{2,1,0:T(8,128)(2,1)S(1)}, u32[]{:S(2)}, u32[]{:S(2)}) %collective-permute-start.9) | collective-permute-done | bytes 327712 | tf_op jit(solution)/shard_map/ppermute | solution.py:42
  126.8 2.5 %turn_3_0.1.refs_0_ = bf16[4,64,1280]{2,1,0:T(8,128)(2,1)} custom-call(s32[40]{0:T(128)} %plan.1.table_ref, bf16[8,64,1280]{2,1,0:T(8,128)(2,1)} %get-tuple-element.44.old_ref, bf16[2,64,1280]{2,1,0:T(8,128)(2,1)} %copy-done.4, bf16[2,64,1280]{2,1,0:T(8,128)(2,1)} %copy-done.8, bf16[2,64,1280]{2,1,0:T(8,128)(2,1)} %copy-done.9), custom_call_target="tpu_custom_call" | custom-call | tf_op jit(solution)/shard_map/turn_3_0/pallas_call | solution.py:168
  130.3 2.8 %turn_3_1.1.refs_1_ = bf16[4,72,1280]{2,1,0:T(8,128)(2,1)} custom-call(s32[40]{0:T(128)} %plan.1.table_ref, bf16[8,72,1280]{2,1,0:T(8,128)(2,1)} %get-tuple-element.58.old_ref, bf16[2,72,1280]{2,1,0:T(8,128)(2,1)} %copy-done.1, bf16[2,72,1280]{2,1,0:T(8,128)(2,1)} %copy-done.2, bf16[2,72,1280]{2,1,0:T(8,128)(2,1)} %copy-done.3), custom_call_target="tpu_custom_call" | custom-call | tf_op jit(solution)/shard_map/turn_3_1/pallas_call | solution.py:168
  133.1 36.1 %layer.1 = (bf16[512,1280]{1,0:T(8,128)(2,1)}, bf16[64,200,128]{2,1,0:T(8,128)(2,1)}, bf16[64,200,128]{2,1,0:T(8,128)(2,1)}) custom-call(s32[40]{0:T(128)} %plan.1.table_ref, bf16[4,64,1280]{2,1,0:T(8,128)(2,1)} %turn_3_0.1.refs_0_, bf16[4,72,1280]{2,1,0:T(8,128)(2,1)} %turn_3_1.1.refs_1_, bf16[32,1280]{1,0:T(8,128)(2,1)} %pad_maximum_fusion.2.refs_2_, ...), custom_call_target="tpu_custom_call" | custom-call | tf_op jit(solution)/shard_map/layer/pallas_call | solution.py:426
  171.2 5.7 %collective-permute-done.20 = bf16[64,200,128]{2,1,0:T(8,128)(2,1)S(1)} collective-permute-done((bf16[64,200,128]{2,1,0:T(8,128)(2,1)}, bf16[64,200,128]{2,1,0:T(8,128)(2,1)S(1)}, u32[]{:S(2)}, u32[]{:S(2)}) %collective-permute-start.20) | collective-permute-done | bytes 3276832 | tf_op jit(solution)/shard_map/ppermute | solution.py:485
  176.9 2.8 %add_convert_fusion = bf16[64,200,128]{2,1,0:T(8,128)(2,1)S(1)} fusion(bf16[64,200,128]{2,1,0:T(8,128)(2,1)S(1)} %collective-permute-done.20, bf16[64,200,128]{2,1,0:T(8,128)(2,1)} %get-tuple-element.63), kind=kLoop, calls=%fused_computation.2 | loop fusion | flops 6553600 | bytes 9830400 | tf_op jit(solution)/shard_map/convert_element_type | solution.py:486
  179.7 45.2 %all_to_all.5 = bf16[64,200,128]{2,1,0:T(8,128)(2,1)S(1)} all-to-all(bf16[64,200,128]{2,1,0:T(8,128)(2,1)S(1)} %add_convert_fusion), channel_id=1, replica_groups={{0,2,4,6,8,10,12,14,16,18,20,22,24,26,28,30,32,34,36,38,40,42,44,46,48,..., dimensions={0} | all-to-all | bytes 6553600 | tf_op jit(solution)/shard_map/all_to_all | solution.py:487
  (105 shorter events, 37.2 us)
Async XLA Ops:
  5.1 16.9 %collective-permute-start.10 = (bf16[2,72,1280]{2,1,0:T(8,128)(2,1)}, bf16[2,72,1280]{2,1,0:T(8,128)(2,1)S(1)}, u32[]{:S(2)}, u32[]{:S(2)}) collective-permute-start(bf16[2,72,1280]{2,1,0:T(8,128)(2,1)} %get-tuple-element.49), channel_id=1, source_target_pairs={{0,1},{1,0},{2,3},{3,2},{4,5},{5,4},{6,7},{7,6},{8,9},{9,8},{10,11... | collective-permute-start | bytes 1105928 | tf_op jit(solution)/shard_map/ppermute | solution.py:42
  11.4 1.9 collective-permute-start
  16.9 12.7 %collective-permute-start.1 = (bf16[2,64,1280]{2,1,0:T(8,128)(2,1)}, bf16[2,64,1280]{2,1,0:T(8,128)(2,1)S(1)}, u32[]{:S(2)}, u32[]{:S(2)}) collective-permute-start(bf16[2,64,1280]{2,1,0:T(8,128)(2,1)} %get-tuple-element.37), channel_id=1, source_target_pairs={{0,2},{1,3},{2,0},{3,1},{4,6},{5,7},{6,4},{7,5},{8,10},{9,11},{10,... | collective-permute-start | bytes 983048 | tf_op jit(solution)/shard_map/ppermute | solution.py:42
  18.6 18.3 %collective-permute-start.2 = (bf16[2,64,1280]{2,1,0:T(8,128)(2,1)}, bf16[2,64,1280]{2,1,0:T(8,128)(2,1)S(1)}, u32[]{:S(2)}, u32[]{:S(2)}) collective-permute-start(bf16[2,64,1280]{2,1,0:T(8,128)(2,1)} %get-tuple-element.38), channel_id=1, source_target_pairs={{0,4},{1,5},{2,6},{3,7},{4,0},{5,1},{6,2},{7,3},{8,12},{9,13},{10,... | collective-permute-start | bytes 983048 | tf_op jit(solution)/shard_map/ppermute | solution.py:42
  22.0 17.0 %collective-permute-start.3 = (bf16[2,64,1280]{2,1,0:T(8,128)(2,1)}, bf16[2,64,1280]{2,1,0:T(8,128)(2,1)S(1)}, u32[]{:S(2)}, u32[]{:S(2)}) collective-permute-start(bf16[2,64,1280]{2,1,0:T(8,128)(2,1)} %get-tuple-element.39), channel_id=1, source_target_pairs={{0,6},{1,7},{2,4},{3,5},{4,2},{5,3},{6,0},{7,1},{8,14},{9,15},{10,... | collective-permute-start | bytes 983048 | tf_op jit(solution)/shard_map/ppermute | solution.py:42
  25.8 28.8 %collective-permute-start.11 = (bf16[2,72,1280]{2,1,0:T(8,128)(2,1)}, bf16[2,72,1280]{2,1,0:T(8,128)(2,1)}, u32[]{:S(2)}, u32[]{:S(2)}) collective-permute-start(bf16[2,72,1280]{2,1,0:T(8,128)(2,1)} %get-tuple-element.51), channel_id=1, source_target_pairs={{0,2},{1,3},{2,0},{3,1},{4,6},{5,7},{6,4},{7,5},{8,10},{9,11},{10,... | collective-permute-start | bytes 1105928 | tf_op jit(solution)/shard_map/ppermute | solution.py:42
  25.8 29.1 %collective-permute-start.12 = (bf16[2,72,1280]{2,1,0:T(8,128)(2,1)}, bf16[2,72,1280]{2,1,0:T(8,128)(2,1)}, u32[]{:S(2)}, u32[]{:S(2)}) collective-permute-start(bf16[2,72,1280]{2,1,0:T(8,128)(2,1)} %get-tuple-element.52), channel_id=1, source_target_pairs={{0,4},{1,5},{2,6},{3,7},{4,0},{5,1},{6,2},{7,3},{8,12},{9,13},{10,... | collective-permute-start | bytes 1105928 | tf_op jit(solution)/shard_map/ppermute | solution.py:42
  29.6 25.3 %collective-permute-start.13 = (bf16[2,72,1280]{2,1,0:T(8,128)(2,1)}, bf16[2,72,1280]{2,1,0:T(8,128)(2,1)}, u32[]{:S(2)}, u32[]{:S(2)}) collective-permute-start(bf16[2,72,1280]{2,1,0:T(8,128)(2,1)} %get-tuple-element.53), channel_id=1, source_target_pairs={{0,6},{1,7},{2,4},{3,5},{4,2},{5,3},{6,0},{7,1},{8,14},{9,15},{10,... | collective-permute-start | bytes 1105928 | tf_op jit(solution)/shard_map/ppermute | solution.py:42
  42.8 19.0 %collective-permute-start.4 = (bf16[2,64,1280]{2,1,0:T(8,128)(2,1)}, bf16[2,64,1280]{2,1,0:T(8,128)(2,1)}, u32[]{:S(2)}, u32[]{:S(2)}) collective-permute-start(bf16[2,64,1280]{2,1,0:T(8,128)(2,1)} %get-tuple-element.41), channel_id=1, source_target_pairs={{0,8},{1,9},{2,10},{3,11},{4,12},{5,13},{6,14},{7,15},{8,0},{9,1},... | collective-permute-start | bytes 983048 | tf_op jit(solution)/shard_map/ppermute | solution.py:42
  52.2 16.0 %collective-permute-start.5 = (bf16[2,64,1280]{2,1,0:T(8,128)(2,1)}, bf16[2,64,1280]{2,1,0:T(8,128)(2,1)}, u32[]{:S(2)}, u32[]{:S(2)}) collective-permute-start(bf16[2,64,1280]{2,1,0:T(8,128)(2,1)} %get-tuple-element.42), channel_id=1, source_target_pairs={{0,16},{1,17},{2,18},{3,19},{4,20},{5,21},{6,22},{7,23},{8,24},{9,... | collective-permute-start | bytes 983048 | tf_op jit(solution)/shard_map/ppermute | solution.py:42
  54.6 18.6 %collective-permute-start.6 = (bf16[2,64,1280]{2,1,0:T(8,128)(2,1)}, bf16[2,64,1280]{2,1,0:T(8,128)(2,1)}, u32[]{:S(2)}, u32[]{:S(2)}) collective-permute-start(bf16[2,64,1280]{2,1,0:T(8,128)(2,1)} %get-tuple-element.43), channel_id=1, source_target_pairs={{0,24},{1,25},{2,26},{3,27},{4,28},{5,29},{6,30},{7,31},{8,16},{9,... | collective-permute-start | bytes 983048 | tf_op jit(solution)/shard_map/ppermute | solution.py:42
  58.2 20.1 %collective-permute-start.14 = (bf16[2,72,1280]{2,1,0:T(8,128)(2,1)}, bf16[2,72,1280]{2,1,0:T(8,128)(2,1)}, u32[]{:S(2)}, u32[]{:S(2)}) collective-permute-start(bf16[2,72,1280]{2,1,0:T(8,128)(2,1)} %get-tuple-element.55), channel_id=1, source_target_pairs={{0,8},{1,9},{2,10},{3,11},{4,12},{5,13},{6,14},{7,15},{8,0},{9,1},... | collective-permute-start | bytes 1105928 | tf_op jit(solution)/shard_map/ppermute | solution.py:42
  59.4 18.9 %collective-permute-start.15 = (bf16[2,72,1280]{2,1,0:T(8,128)(2,1)}, bf16[2,72,1280]{2,1,0:T(8,128)(2,1)}, u32[]{:S(2)}, u32[]{:S(2)}) collective-permute-start(bf16[2,72,1280]{2,1,0:T(8,128)(2,1)} %get-tuple-element.56), channel_id=1, source_target_pairs={{0,16},{1,17},{2,18},{3,19},{4,20},{5,21},{6,22},{7,23},{8,24},{9,... | collective-permute-start | bytes 1105928 | tf_op jit(solution)/shard_map/ppermute | solution.py:42
  61.8 24.6 %collective-permute-start.16 = (bf16[2,72,1280]{2,1,0:T(8,128)(2,1)}, bf16[2,72,1280]{2,1,0:T(8,128)(2,1)}, u32[]{:S(2)}, u32[]{:S(2)}) collective-permute-start(bf16[2,72,1280]{2,1,0:T(8,128)(2,1)} %get-tuple-element.57), channel_id=1, source_target_pairs={{0,24},{1,25},{2,26},{3,27},{4,28},{5,29},{6,30},{7,31},{8,16},{9,... | collective-permute-start | bytes 1105928 | tf_op jit(solution)/shard_map/ppermute | solution.py:42
  68.2 28.3 %copy-start.13 = (bf16[1920]{0:T(1024)(128)(2,1)S(1)}, bf16[1920]{0:T(1024)(128)(2,1)}, u32[]{:S(2)}) copy-start(bf16[1920]{0:T(1024)(128)(2,1)} %param.22) | copy-start | bytes 11524
  73.2 26.2 %copy-start.16 = (bf16[1280]{0:T(1024)(128)(2,1)S(1)}, bf16[1280]{0:T(1024)(128)(2,1)}, u32[]{:S(2)}) copy-start(bf16[1280]{0:T(1024)(128)(2,1)} %param.24) | copy-start | bytes 7684
  76.3 19.1 %collective-permute-start.7 = (bf16[2,64,1280]{2,1,0:T(8,128)(2,1)}, bf16[2,64,1280]{2,1,0:T(8,128)(2,1)S(1)}, u32[]{:S(2)}, u32[]{:S(2)}) collective-permute-start(bf16[2,64,1280]{2,1,0:T(8,128)(2,1)} %get-tuple-element.45), channel_id=1, source_target_pairs={{0,32},{1,33},{2,34},{3,35},{4,36},{5,37},{6,38},{7,39},{8,40},{9,... | collective-permute-start | bytes 983048 | tf_op jit(solution)/shard_map/ppermute | solution.py:42
  89.7 39.5 %collective-permute-start.17 = (bf16[2,72,1280]{2,1,0:T(8,128)(2,1)}, bf16[2,72,1280]{2,1,0:T(8,128)(2,1)S(1)}, u32[]{:S(2)}, u32[]{:S(2)}) collective-permute-start(bf16[2,72,1280]{2,1,0:T(8,128)(2,1)} %get-tuple-element.59), channel_id=1, source_target_pairs={{0,32},{1,33},{2,34},{3,35},{4,36},{5,37},{6,38},{7,39},{8,40},{9,... | collective-permute-start | bytes 1105928 | tf_op jit(solution)/shard_map/ppermute | solution.py:42
  91.0 38.3 %collective-permute-start.18 = (bf16[2,72,1280]{2,1,0:T(8,128)(2,1)}, bf16[2,72,1280]{2,1,0:T(8,128)(2,1)S(1)}, u32[]{:S(2)}, u32[]{:S(2)}) collective-permute-start(bf16[2,72,1280]{2,1,0:T(8,128)(2,1)} %get-tuple-element.60), channel_id=1, source_target_pairs={{0,64},{1,65},{2,66},{3,67},{4,68},{5,69},{6,70},{7,71},{8,72},{9,... | collective-permute-start | bytes 1105928 | tf_op jit(solution)/shard_map/ppermute | solution.py:42
  93.6 35.7 %collective-permute-start.19 = (bf16[2,72,1280]{2,1,0:T(8,128)(2,1)}, bf16[2,72,1280]{2,1,0:T(8,128)(2,1)S(1)}, u32[]{:S(2)}, u32[]{:S(2)}) collective-permute-start(bf16[2,72,1280]{2,1,0:T(8,128)(2,1)} %get-tuple-element.61), channel_id=1, source_target_pairs={{0,96},{1,97},{2,98},{3,99},{4,100},{5,101},{6,102},{7,103},{8,104... | collective-permute-start | bytes 1105928 | tf_op jit(solution)/shard_map/ppermute | solution.py:42
  93.7 23.2 %collective-permute-start.8 = (bf16[2,64,1280]{2,1,0:T(8,128)(2,1)}, bf16[2,64,1280]{2,1,0:T(8,128)(2,1)S(1)}, u32[]{:S(2)}, u32[]{:S(2)}) collective-permute-start(bf16[2,64,1280]{2,1,0:T(8,128)(2,1)} %get-tuple-element.46), channel_id=1, source_target_pairs={{0,64},{1,65},{2,66},{3,67},{4,68},{5,69},{6,70},{7,71},{8,72},{9,... | collective-permute-start | bytes 983048 | tf_op jit(solution)/shard_map/ppermute | solution.py:42
  95.4 30.7 %copy-start.4 = (bf16[2,64,1280]{2,1,0:T(8,128)(2,1)}, bf16[2,64,1280]{2,1,0:T(8,128)(2,1)S(1)}, u32[]{:S(2)}) copy-start(bf16[2,64,1280]{2,1,0:T(8,128)(2,1)S(1)} %collective-permute-done.7.rest_0_) | copy-start | bytes 983044
  95.4 30.7 %collective-permute-start.9 = (bf16[2,64,1280]{2,1,0:T(8,128)(2,1)}, bf16[2,64,1280]{2,1,0:T(8,128)(2,1)S(1)}, u32[]{:S(2)}, u32[]{:S(2)}) collective-permute-start(bf16[2,64,1280]{2,1,0:T(8,128)(2,1)} %get-tuple-element.47), channel_id=1, source_target_pairs={{0,96},{1,97},{2,98},{3,99},{4,100},{5,101},{6,102},{7,103},{8,104... | collective-permute-start | bytes 983048 | tf_op jit(solution)/shard_map/ppermute | solution.py:42
  169.2 7.7 %collective-permute-start.20 = (bf16[64,200,128]{2,1,0:T(8,128)(2,1)}, bf16[64,200,128]{2,1,0:T(8,128)(2,1)S(1)}, u32[]{:S(2)}, u32[]{:S(2)}) collective-permute-start(bf16[64,200,128]{2,1,0:T(8,128)(2,1)} %get-tuple-element.64), channel_id=1, source_target_pairs={{0,1},{1,0},{2,3},{3,2},{4,5},{5,4},{6,7},{7,6},{8,9},{9,8},{10,11... | collective-permute-start | bytes 9830408 | tf_op jit(solution)/shard_map/ppermute | solution.py:485
  (14 other events, 107.8 us)

commit v2 on v1

--- a/solution.py
+++ b/solution.py
@@ -8,6 +8,7 @@
 from jax.experimental.pallas import tpu as pltpu
 from jax.sharding import PartitionSpec as P
 
+
 HEAD = 80
 BLOCK = 128
 EPSILON = 1e-06
@@ -19,6 +20,8 @@
 WINDOW = 2
 GROUPS = ((0,), (1, 2), (3, 4), (5, 6))
 FIELDS = 8
+PAD = 4
+SMALL = 10 * 1024 * 1024
 
 SMEM = pl.BlockSpec(memory_space=pltpu.SMEM)
 VMEM = pl.BlockSpec(memory_space=pltpu.VMEM)
@@ -38,13 +41,13 @@
 
 def exchange(values, group):
     size = lax.axis_size(AXIS)
-    return [
-        lax.ppermute(value, AXIS, [(i, i ^ mask) for i in range(size)])
-        for value, mask in zip(values, masks_of(group))
-    ]
-
-
-def plan_kernel(counts_ref, sends_ref, table_ref):
+    out = []
+    for value, mask in zip(values, masks_of(group)):
+        out.append(lax.ppermute(value, AXIS, [(i, i ^ mask) for i in range(size)]))
+    return out
+
+
+def plan(counts_ref, sends_ref, table_ref):
     me = lax.axis_index(AXIS)
     count = counts_ref[me]
     for group, sections in enumerate(GROUPS):
@@ -78,16 +81,6 @@
     table_ref[len(GROUPS) * FIELDS] = count
 
 
-def make_plan(block_counts, send_counts):
-    return pl.pallas_call(
-        plan_kernel,
-        out_shape=jax.ShapeDtypeStruct((len(GROUPS) * FIELDS + 8,), jnp.int32),
-        in_specs=[SMEM, SMEM],
-        out_specs=SMEM,
-        name="plan",
-    )(block_counts, send_counts)
-
-
 def cut(table_ref, stack_ref, window_refs, group):
     for which, window_ref in enumerate(window_refs):
         low = table_ref[group * FIELDS + which]
@@ -95,15 +88,18 @@
             window_ref[i] = stack_ref[low + i]
 
 
-def land(table_ref, stack_ref, far_refs, group):
+def landings(table_ref, group):
     base = group * FIELDS
     floor = table_ref[base + 5]
-    targets = (
+    return (
         (table_ref[base + 3], table_ref[base + 4]),
         (floor, table_ref[base + 6]),
         (floor + table_ref[base + 6], table_ref[base + 7]),
     )
-    for far_ref, (start, total) in zip(far_refs, targets):
+
+
+def land(table_ref, stack_ref, far_refs, group):
+    for far_ref, (start, total) in zip(far_refs, landings(table_ref, group)):
         for i in range(WINDOW):
 
             @pl.when(i < total)
@@ -111,42 +107,57 @@
                 stack_ref[start + i] = far_ref[i]
 
 
-def open_kernel(piece, begin, table_ref, patches_ref, *rest):
-    if piece == 0:
-        grids_ref, stack_ref, window_ref, sem = rest
-    else:
-        stack_ref, window_ref, sem = rest
-    rows = PIECES[piece]
+def open_kernel(counts_ref, sends_ref, grids_ref, patches_ref, table_ref, *rest):
+    pieces = len(PIECES)
+    stack_refs, window_refs, sems = rest[:pieces], rest[pieces : 2 * pieces], rest[2 * pieces]
     slots = patches_ref.shape[0]
-    copy = pltpu.make_async_copy(
-        patches_ref.at[:, pl.ds(begin, rows)], stack_ref.at[pl.ds(0, slots), pl.ds(0, rows)], sem
-    )
-    copy.start()
-    for slot in range(slots, STACK):
-        stack_ref[slot] = jnp.zeros(stack_ref.shape[1:], stack_ref.dtype)
-    if piece == 0:
-        for slot in range(slots):
-            stack_ref[slot, rows:, :] = grids_ref[slot]
-    copy.wait()
-    cut(table_ref, stack_ref, (window_ref,), 0)
-
-
-def open_piece(table, patches, grids, piece):
-    rows = payload_rows(piece)
+    copies, begin = [], 0
+    for piece, rows in enumerate(PIECES):
+        copies.append(
+            pltpu.make_async_copy(
+                patches_ref.at[:, pl.ds(begin, rows)],
+                stack_refs[piece].at[pl.ds(0, slots), pl.ds(0, rows)],
+                sems.at[piece],
+            )
+        )
+        copies[-1].start()
+        begin += rows
+    plan(counts_ref, sends_ref, table_ref)
+    for stack_ref in stack_refs:
+        for slot in range(slots, STACK):
+            stack_ref[slot] = jnp.zeros(stack_ref.shape[1:], stack_ref.dtype)
+    numbers = grids_ref.shape[1] * grids_ref.shape[2]
+    lane = lax.broadcasted_iota(jnp.int32, (MARK, 128), 1)
+    for slot in range(slots):
+        marks = jnp.zeros((MARK, 128), jnp.float32)
+        for k in range(numbers):
+            number = grids_ref[slot, k // 2, k % 2].astype(jnp.float32)
+            marks = jnp.where(lane == k, number, marks)
+        stack_refs[0][slot, PIECES[0] :, :128] = marks.astype(jnp.bfloat16)
+        stack_refs[0][slot, PIECES[0] :, 128:] = jnp.zeros(
+            (MARK, stack_refs[0].shape[2] - 128), jnp.bfloat16
+        )
+    for piece in range(pieces):
+        copies[piece].wait()
+        cut(table_ref, stack_refs[piece], (window_refs[piece],), 0)
+
+
+def open_pieces(block_counts, send_counts, patch_grids, patches):
     width = patches.shape[-1]
-    begin = sum(PIECES[:piece])
-    extra = (grids,) if piece == 0 else ()
-    return pl.pallas_call(
-        functools.partial(open_kernel, piece, begin),
-        out_shape=(
-            jax.ShapeDtypeStruct((STACK, rows, width), patches.dtype),
-            jax.ShapeDtypeStruct((WINDOW, rows, width), patches.dtype),
-        ),
-        in_specs=[SMEM, pl.BlockSpec(memory_space=pl.ANY)] + [VMEM] * len(extra),
-        out_specs=(VMEM, VMEM),
-        scratch_shapes=[pltpu.SemaphoreType.DMA],
-        name=f"open_{piece}",
-    )(table, patches, *extra)
+    heights = [payload_rows(piece) for piece in range(len(PIECES))]
+    out = pl.pallas_call(
+        open_kernel,
+        out_shape=(jax.ShapeDtypeStruct((len(GROUPS) * FIELDS + 8,), jnp.int32),)
+        + tuple(jax.ShapeDtypeStruct((STACK, rows, width), patches.dtype) for rows in heights)
+        + tuple(jax.ShapeDtypeStruct((WINDOW, rows, width), patches.dtype) for rows in heights),
+        in_specs=[SMEM, SMEM, SMEM, pl.BlockSpec(memory_space=pltpu.HBM)],
+        out_specs=(SMEM,) + (VMEM,) * (2 * len(PIECES)),
+        scratch_shapes=[pltpu.SemaphoreType.DMA((len(PIECES),))],
+        compiler_params=pltpu.CompilerParams(vmem_limit_bytes=SMALL),
+        name="open",
+    )(block_counts, send_counts, patch_grids, patches)
+    count = len(PIECES)
+    return out[0], list(out[1 : 1 + count]), [[window] for window in out[1 + count :]]
 
 
 def turn_kernel(group, table_ref, old_ref, *rest):
@@ -154,50 +165,36 @@
     fars = rest[:far_count]
     stack_ref = rest[far_count]
     windows = rest[far_count + 1 :]
-    stack_ref[...] = old_ref[: stack_ref.shape[0]]
+    stack_ref[...] = old_ref[...]
     land(table_ref, stack_ref, fars, group)
-    if windows:
-        cut(table_ref, stack_ref, windows, group + 1)
-
-
-def turn(table, stack, fars, group, piece, balanced):
-    last = group == len(GROUPS) - 1
-    slots = balanced if last else STACK
+    cut(table_ref, stack_ref, windows, group + 1)
+
+
+def turn(table, stack, fars, group):
     window = jax.ShapeDtypeStruct((WINDOW,) + stack.shape[1:], stack.dtype)
-    sends = 0 if last else len(masks_of(group + 1))
+    sends = len(masks_of(group + 1))
     out = pl.pallas_call(
         functools.partial(turn_kernel, group),
-        out_shape=(jax.ShapeDtypeStruct((slots,) + stack.shape[1:], stack.dtype),) + (window,) * sends,
+        out_shape=(jax.ShapeDtypeStruct(stack.shape, stack.dtype),) + (window,) * sends,
         in_specs=[SMEM, VMEM] + [VMEM] * len(fars),
         out_specs=(VMEM,) * (1 + sends),
-        name=f"turn_{group}_{piece}",
+        compiler_params=pltpu.CompilerParams(vmem_limit_bytes=SMALL),
     )(table, stack, *fars)
     return out[0], list(out[1:])
 
 
-def balance(patches, patch_grids, table, balanced):
+def balance(patches, patch_grids, block_counts, send_counts):
     slots = patch_grids.shape[0]
-    width = patches.shape[-1]
-    blocks = patches.reshape(slots, BLOCK, width)
-    grids = jnp.broadcast_to(
-        jnp.pad(
-            patch_grids.reshape(slots, 1, -1).astype(jnp.bfloat16),
-            ((0, 0), (0, 0), (0, width - patch_grids[0].size)),
-        ),
-        (slots, MARK, width),
-    )
-    stacks, windows = [], []
-    for piece in range(len(PIECES)):
-        stack, window = open_piece(table, blocks, grids, piece)
-        stacks.append(stack)
-        windows.append([window])
+    blocks = patches.reshape(slots, BLOCK, patches.shape[-1])
+    table, stacks, windows = open_pieces(block_counts, send_counts, patch_grids, blocks)
     for group in range(len(GROUPS)):
         for piece in range(len(PIECES)):
             fars = exchange(windows[piece], group)
-            stacks[piece], windows[piece] = turn(
-                table, stacks[piece], fars, group, piece, balanced
-            )
-    return stacks
+            if group == len(GROUPS) - 1:
+                stacks[piece] = [stacks[piece]] + fars
+                continue
+            stacks[piece], windows[piece] = turn(table, stacks[piece], fars, group)
+    return table, stacks
 
 
 def dot_nt(a, b):
@@ -236,20 +233,23 @@
     *refs,
 ):
     pieces = len(PIECES)
-    stack_refs = refs[:pieces]
+    group = len(GROUPS) - 1
+    each = 1 + len(masks_of(group))
+    arrivals = [refs[piece * each : (piece + 1) * each] for piece in range(pieces)]
     (
         levels_ref,
         gain_ref,
         bias_ref,
-        wall_hbm,
-        ball_ref,
+        w_turned_hbm,
+        turn_qkv_hbm,
+        b_qkv_ref,
         w_out_hbm,
-        turn_out_ref,
+        turn_out_hbm,
         b_out_ref,
         cot_hbm,
-        result_ref,
-        given_ref,
-        kept_ref,
+        result_hbm,
+        given_hbm,
+        kept_hbm,
         x_ref,
         normed_ref,
         mixed_ref,
@@ -260,35 +260,77 @@
         lines_ref,
         seg_row_ref,
         seg_col_ref,
-        wall_ref,
+        w_turned_ref,
+        turn_qkv_ref,
         w_out_ref,
+        turn_out_ref,
         cot_ref,
+        result_ref,
+        given_ref,
+        kept_ref,
         sems,
-    ) = refs[pieces:]
-    balanced = stack_refs[0].shape[0]
+        raw_sems,
+        out_sems,
+        *raw_refs,
+    ) = refs[pieces * each :]
+    balanced = raw_refs[0].shape[0]
     width = x_ref.shape[1]
-    tokens = balanced * BLOCK
     inner = w_out_ref.shape[0]
     heads = inner // HEAD
     live_count = table_ref[len(GROUPS) * FIELDS]
     images = 4
+    spots = landings(table_ref, group)
+    raws = []
+    for piece in range(pieces):
+        for slot in range(balanced):
+            stays = pltpu.make_async_copy(
+                arrivals[piece][0].at[slot], raw_refs[piece].at[slot], raw_sems.at[piece]
+            )
+            raws.append(stays)
+            home = jnp.bool_(True)
+            for far, (start, total) in zip(arrivals[piece][1:], spots):
+                here = (slot >= start) & (slot < start + total)
+                home = home & jnp.logical_not(here)
+                source = jnp.clip(slot - start, 0, WINDOW - 1)
+
+                @pl.when(here)
+                def _():
+                    pltpu.make_async_copy(
+                        far.at[source], raw_refs[piece].at[slot], raw_sems.at[piece]
+                    ).start()
+
+            pl.when(home)(stays.start)
     copies = [
         pltpu.make_async_copy(src, dst, sems.at[i])
         for i, (src, dst) in enumerate(
-            ((cot_hbm, cot_ref), (w_out_hbm, w_out_ref), (wall_hbm, wall_ref))
+            (
+                (cot_hbm, cot_ref),
+                (w_out_hbm, w_out_ref),
+                (w_turned_hbm, w_turned_ref),
+                (turn_qkv_hbm, turn_qkv_ref),
+                (turn_out_hbm, turn_out_ref),
+            )
         )
     ]
     for copy in copies:
         copy.start()
+    leaving = [
+        pltpu.make_async_copy(src, dst, out_sems.at[i])
+        for i, (src, dst) in enumerate(
+            ((result_ref, result_hbm), (given_ref, given_hbm), (kept_ref, kept_hbm))
+        )
+    ]
 
     col = lax.broadcasted_iota(jnp.int32, (BLOCK, 1), 0).astype(jnp.float32)
     lane = lax.broadcasted_iota(jnp.int32, (1, BLOCK), 1).astype(jnp.float32)
     level = lax.broadcasted_iota(jnp.int32, (BLOCK, levels_ref.shape[0]), 1).astype(jnp.float32)
     half = float(levels_ref.shape[0] // 2)
 
+    for raw in raws:
+        raw.wait()
     for slot in range(balanced):
         at = slot * BLOCK
-        grid = stack_refs[0][slot, PIECES[0] : PIECES[0] + MARK, :BLOCK].astype(jnp.float32)
+        grid = raw_refs[0][slot, PIECES[0] : PIECES[0] + MARK, :BLOCK].astype(jnp.float32)
         grid = grid[0:1, : 2 * images]
         segment, row, column, inside = image_of_tokens(grid, col)
         seg_col_ref[at : at + BLOCK, :] = segment
@@ -299,7 +341,7 @@
         emb = dot_nn(hot.astype(jnp.bfloat16), levels_ref[...])
         begin = 0
         for piece, rows in enumerate(PIECES):
-            raw = stack_refs[piece][slot, :rows, :].astype(jnp.float32)
+            raw = raw_refs[piece][slot, :rows, :].astype(jnp.float32)
             x_ref[at + begin : at + begin + rows, :] = (
                 raw + emb[begin : begin + rows, :]
             ).astype(jnp.bfloat16)
@@ -322,9 +364,14 @@
     attn_grad_ref[...] = dot_nt(w_out_ref[...], out_grad_ref[...]).astype(jnp.bfloat16)
     copies[2].wait()
     step = 640
-    for at in range(0, wall_ref.shape[0], step):
+    for at in range(0, 3 * inner, step):
         mixed_ref[at : at + step, :] = (
-            dot_nt(wall_ref[at : at + step, :], normed_ref[...]) + ball_ref[at : at + step, :]
+            dot_nt(w_turned_ref[at : at + step, :], normed_ref[...]) + b_qkv_ref[at : at + step, :]
+        ).astype(jnp.bfloat16)
+    copies[3].wait()
+    for at in range(0, width, step):
+        mixed_ref[3 * inner + at : 3 * inner + at + step, :] = dot_nt(
+            turn_qkv_ref[at : at + step, :], normed_ref[...]
         ).astype(jnp.bfloat16)
 
     scale = 1.0 / math.sqrt(HEAD)
@@ -366,8 +413,11 @@
             jnp.bfloat16
         )
 
+    leaving[0].start()
+    copies[4].wait()
     turned = dot_nn(turn_out_ref[...], attended_ref[...]).astype(jnp.bfloat16)
     chips = given_ref.shape[0]
+    pitch = chips + PAD
     qkv_tiles = 3 * inner // 128
     out_tiles = width // 128
     per_rank = width // (2 * chips)
@@ -389,14 +439,14 @@
                     :, t * 128 : (t + 1) * 128
                 ].reshape(chips, 8, 128)
                 for e in range(rest):
-                    line = ((tile + t) * rest + e) * chips
+                    line = ((tile + t) * rest + e) * pitch
                     lines_ref[line : line + chips, :] = side[
                         e * chips : (e + 1) * chips, t * 128 : (t + 1) * 128
                     ]
         block = dot_nn(turned[part * out_rank * chips : (part + 1) * out_rank * chips, :], out_grad_ref[...])
         for t in range(out_tiles):
             for e in range(out_rank):
-                line = (qkv_tiles * rest + t * out_rank + e) * chips
+                line = (qkv_tiles * rest + t * out_rank + e) * pitch
                 lines_ref[line : line + chips, :] = block[
                     e * chips : (e + 1) * chips, t * 128 : (t + 1) * 128
                 ]
@@ -404,16 +454,21 @@
 
         def one_chip(chip, carry):
             for b in range(count // 8):
-                lines = lines_ref[pl.ds(chip + b * 8 * chips, 8, stride=chips), :]
+                lines = lines_ref[pl.ds(chip + b * 8 * pitch, 8, stride=pitch), :]
                 target[chip, 8 * qkv_tiles + 8 * b : 8 * qkv_tiles + 8 * b + 8, :] = lines.astype(
                     jnp.bfloat16
                 )
             return carry
 
-        lax.fori_loop(0, chips, one_chip, 0)
-
-
-def layer(table, stacks, levels, gain, bias, wall, ball, w_out, turn_out, b_out, cotangent):
+        lax.fori_loop(0, chips, one_chip, 0, unroll=8)
+        leaving[1 + part].start()
+    for copy in leaving:
+        copy.wait()
+
+
+def layer(
+    table, stacks, levels, gain, bias, w_turned, turn_qkv, b_qkv, w_out, turn_out, b_out, cotangent
+):
     width = cotangent.shape[1]
     tokens = cotangent.shape[0]
     balanced = tokens // BLOCK
@@ -421,7 +476,7 @@
     chips = lax.axis_size(AXIS) // 2
     lines = (width // (2 * chips) * 3 * inner + inner // (2 * chips) * width) // 128
     any_space = pl.BlockSpec(memory_space=pl.ANY)
-    first = [VMEM] * len(stacks)
+    arrived = [array for piece in stacks for array in piece]
     bf16, f32 = jnp.bfloat16, jnp.float32
     return pl.pallas_call(
         layer_kernel,
@@ -431,28 +486,68 @@
             jax.ShapeDtypeStruct((chips, lines, 128), bf16),
         ),
         in_specs=[SMEM]
-        + first
-        + [VMEM, VMEM, VMEM, any_space, VMEM, any_space, VMEM, VMEM, any_space],
-        out_specs=(VMEM, VMEM, VMEM),
+        + [any_space] * len(arrived)
+        + [VMEM, VMEM, VMEM, any_space, any_space, VMEM, any_space, any_space, VMEM, any_space],
+        out_specs=(any_space,) * 3,
         scratch_shapes=[
             pltpu.VMEM((tokens, width), bf16),
             pltpu.VMEM((tokens, width), bf16),
-            pltpu.VMEM((wall.shape[0], tokens), bf16),
+            pltpu.VMEM((3 * inner + width, tokens), bf16),
             pltpu.VMEM((3 * inner, tokens), bf16),
             pltpu.VMEM((inner, tokens), bf16),
             pltpu.VMEM((tokens, width), bf16),
             pltpu.VMEM((inner, tokens), bf16),
-            pltpu.VMEM(((lines - 8 * (3 * inner // 128)) * chips, 128), f32),
+            pltpu.VMEM(((lines - 8 * (3 * inner // 128)) * (chips + PAD), 128), f32),
             pltpu.VMEM((balanced, 8, BLOCK), f32),
             pltpu.VMEM((tokens, 1), f32),
-            pltpu.VMEM(wall.shape, bf16),
+            pltpu.VMEM(w_turned.shape, bf16),
+            pltpu.VMEM(turn_qkv.shape, bf16),
             pltpu.VMEM(w_out.shape, bf16),
+            pltpu.VMEM(turn_out.shape, bf16),
             pltpu.VMEM(cotangent.shape, bf16),
+            pltpu.VMEM((tokens, width), bf16),
+            pltpu.VMEM((chips, lines, 128), bf16),
+            pltpu.VMEM((chips, lines, 128), bf16),
+            pltpu.SemaphoreType.DMA((5,)),
+            pltpu.SemaphoreType.DMA((len(PIECES),)),
             pltpu.SemaphoreType.DMA((3,)),
+        ]
+        + [
+            pltpu.VMEM((balanced, payload_rows(piece), width), bf16)
+            for piece in range(len(PIECES))
         ],
-        compiler_params=pltpu.CompilerParams(vmem_limit_bytes=60 * 1024 * 1024),
+        compiler_params=pltpu.CompilerParams(vmem_limit_bytes=48 * 1024 * 1024),
         name="layer",
-    )(table, *stacks, levels, gain, bias, wall, ball, w_out, turn_out, b_out, cotangent)
+    )(
+        table,
+        *arrived,
+        levels,
+        gain,
+        bias,
+        w_turned,
+        turn_qkv,
+        b_qkv,
+        w_out,
+        turn_out,
+        b_out,
+        cotangent,
+    )
+
+
+def turn_over_kernel(w_ref, out_ref):
+    for at in range(0, w_ref.shape[1], 128):
+        out_ref[at : at + 128, :] = w_ref[:, at : at + 128].T
+
+
+def turned(w):
+    return pl.pallas_call(
+        turn_over_kernel,
+        out_shape=jax.ShapeDtypeStruct(w.shape[::-1], w.dtype),
+        in_specs=[VMEM],
+        out_specs=VMEM,
+        compiler_params=pltpu.CompilerParams(vmem_limit_bytes=2 * SMALL),
+        name="turn_over",
+    )(w)
 
 
 def row_orders(width, inner):
@@ -512,21 +607,22 @@
     cotangent,
 ):
     width, inner = cotangent.shape[1], w_out.shape[0]
-    table = make_plan(block_counts, send_counts)
     qkv_order, out_order = row_orders(width, inner)
-    wall = jnp.concatenate([w_qkv.T, hot_rows(qkv_order)], axis=0)
-    ball = jnp.pad(b_qkv.astype(jnp.float32), (0, width)).reshape(-1, 1)
-    stacks = balance(patches, patch_grids, table, cotangent.shape[0] // BLOCK)
+    w_turned = turned(w_qkv)
+    turn_qkv = hot_rows(qkv_order)
+    turn_out = hot_rows(out_order)
+    table, stacks = balance(patches, patch_grids, block_counts, send_counts)
     result, given, kept = layer(
         table,
         stacks,
         jnp.concatenate([row_table, col_table], axis=0),
         ln_gain.astype(jnp.float32).reshape(1, -1),
         ln_bias.astype(jnp.float32).reshape(1, -1),
-        wall,
-        ball,
+        w_turned,
+        turn_qkv,
+        b_qkv.astype(jnp.float32).reshape(-1, 1),
         w_out,
-        hot_rows(out_order),
+        turn_out,
         b_out.astype(jnp.float32).reshape(1, -1),
         cotangent,
     )
@@ -538,21 +634,7 @@
     return jax.shard_map(
         local,
         mesh=mesh,
-        in_specs=(
-            P("dp", None),
-            P("dp", None, None),
-            P(),
-            P(),
-            P(),
-            P(),
-            P(),
-            P(),
-            P(),
-            P(),
-            P(),
-            P(),
-            P("dp", None),
-        ),
-        out_specs=(P("dp", None), P("dp", None), P("dp", None)),
+        in_specs=(P(AXIS, None), P(AXIS, None, None)) + (P(),) * 10 + (P(AXIS, None),),
+        out_specs=(P(AXIS, None), P(AXIS, None), P(AXIS, None)),
         check_vma=False,
     )

time: 228 us -> 200 us (0.88)
  Pallas kernels: 67.8 us -> 45.1 us
  other arithmetic: 13.3 us -> 6.63 us
  starting transfers between devices: 28.7 us -> 31.4 us
  waiting for transfers between devices: 53.8 us -> 51.2 us
    pallas_call x8 -> x6, Pallas kernels: 24 us -> 10.6 us  [turn(): pl.pallas_call(functools.partial(turn_kernel, group), out_shape=(jax.Shap...]
    concatenate x1 -> x0, other arithmetic: 6.14 us -> none  [local(): wall = jnp.concatenate([w_qkv.T, hot_rows(qkv_order)], axis=0)]
    unnamed x35 -> x45, local copies, waits for them, and re-layouts: 11.5 us -> 16.7 us
    pallas_call x1, Pallas kernels: 36.1 us -> 31.2 us  [layer(): pl.pallas_call(layer_kernel, out_shape=(jax.ShapeDtypeStruct((tokens, wid...]
    pallas_call x3 -> x2, Pallas kernels: 7.7 us -> 3.32 us  [the longest x1 2 us: open_pieces(): pl.pallas_call(open_kernel, out_shape=(jax.ShapeDtypeStruct((len(GROUPS)...]
    ppermute x20, waiting for transfers between devices: 48.2 us -> 45.5 us  [exchange(): out.append(lax.ppermute(value, AXIS, [(i, i ^ mask) for i in range(size)]))]
    ppermute x1, starting transfers between devices: 2.01 us -> 4.38 us  [spread(): taken = lax.ppermute(given, AXIS, [(i, i ^ 1) for i in range(size)])]
  transfers between devices with their start and end apart: 21 -> 21, of which waited for: 8 -> 10; matrix products, arithmetic and copies ran while one was open for 10% -> 2% of each run, Pallas kernels for 11% -> 6%
where the time goes in v2:
time: 200 us; the launch traced here: 199 us
  waiting for transfers between devices  51.2 us (26%)
  blocking collectives  45.4 us (23%)
  Pallas kernels  45.1 us (23%)
  starting transfers between devices  31.4 us (16%)
  local copies, waits for them, and re-layouts  18.3 us (9%)
  other arithmetic  6.63 us (3%)
    ppermute x20, waiting for transfers between devices, exchange(): out.append(lax.ppermute(value, AXIS, [(i, i ^ mask) for i in range(size)]))  45.5 us
    all_to_all x1, blocking collectives, spread(): lax.all_to_all(pair, AXIS, 0, 0, axis_index_groups=chips_with_my_core(siz...  45.4 us
    pallas_call x1, Pallas kernels, layer(): pl.pallas_call(layer_kernel, out_shape=(jax.ShapeDtypeStruct((tokens, wid...  31.2 us
    ppermute x20, starting transfers between devices, exchange(): out.append(lax.ppermute(value, AXIS, [(i, i ^ mask) for i in range(size)]))  27 us
    unnamed x45, local copies, waits for them, and re-layouts  16.7 us
    pallas_call x6, Pallas kernels, turn(): pl.pallas_call(functools.partial(turn_kernel, group), out_shape=(jax.Shap...  10.6 us
    ppermute x1, waiting for transfers between devices, spread(): taken = lax.ppermute(given, AXIS, [(i, i ^ 1) for i in range(size)])  5.68 us
    ppermute x1, starting transfers between devices, spread(): taken = lax.ppermute(given, AXIS, [(i, i ^ 1) for i in range(size)])  4.38 us
  transfers between devices with their start and end apart: 21, of which 10 were waited for; matrix products, arithmetic and copies ran while one was open for 2% of the time, Pallas kernels for 6%

profile of v2, /device:TPU:1, one launch (start us, length us, event | category | flops | bytes accessed | tf_op | source)
XLA Modules:
  0.0 198.8 jit_solution(16045865664853662824)
XLA Ops:
  4.3 2.0 %open.1 = (s32[40]{0:T(128)S(1)}, bf16[8,64,1280]{2,1,0:T(8,128)(2,1)S(1)}, bf16[8,72,1280]{2,1,0:T(8,128)(2,1)S(1)}, bf16[2,64,1280]{2,1,0:T(8,128)(2,1)}, bf16[2,72,1280]{2,1,0:T(8,128)(2,1)}) custom-call(s32[128]{0:T(128)S(1)} %copy-done.11, s32[7,128]{1,0:T(8,128)S(1)} %copy-done.10, s32[6,4,2]{2,1,0:T(4,128)S(1)} %copy.17.grids_ref, ...), custom_call_target="tpu_custom_call" | custom-call | tf_op jit(solution)/shard_map/open/pallas_call | solution.py:148
  17.9 3.5 %collective-permute-start.2 = (bf16[2,64,1280]{2,1,0:T(8,128)(2,1)}, bf16[2,64,1280]{2,1,0:T(8,128)(2,1)S(1)}, u32[]{:S(2)}, u32[]{:S(2)}) collective-permute-start(bf16[2,64,1280]{2,1,0:T(8,128)(2,1)} %copy-done.15), channel_id=1, source_target_pairs={{0,4},{1,5},{2,6},{3,7},{4,0},{5,1},{6,2},{7,3},{8,12},{9,13},{10,... | collective-permute-start | bytes 983048 | tf_op jit(solution)/shard_map/ppermute | solution.py:46
  21.8 2.1 %collective-permute-start.12 = (bf16[2,72,1280]{2,1,0:T(8,128)(2,1)}, bf16[2,72,1280]{2,1,0:T(8,128)(2,1)S(1)}, u32[]{:S(2)}, u32[]{:S(2)}) collective-permute-start(bf16[2,72,1280]{2,1,0:T(8,128)(2,1)} %copy-done.13), channel_id=1, source_target_pairs={{0,4},{1,5},{2,6},{3,7},{4,0},{5,1},{6,2},{7,3},{8,12},{9,13},{10,... | collective-permute-start | bytes 1105928 | tf_op jit(solution)/shard_map/ppermute | solution.py:46
  24.0 2.0 %collective-permute-start.13 = (bf16[2,72,1280]{2,1,0:T(8,128)(2,1)}, bf16[2,72,1280]{2,1,0:T(8,128)(2,1)}, u32[]{:S(2)}, u32[]{:S(2)}) collective-permute-start(bf16[2,72,1280]{2,1,0:T(8,128)(2,1)} %copy-done.12), channel_id=1, source_target_pairs={{0,6},{1,7},{2,4},{3,5},{4,2},{5,3},{6,0},{7,1},{8,14},{9,15},{10,... | collective-permute-start | bytes 1105928 | tf_op jit(solution)/shard_map/ppermute | solution.py:46
  26.2 14.3 %collective-permute-done.2.rest_1_ = bf16[2,64,1280]{2,1,0:T(8,128)(2,1)S(1)} collective-permute-done((bf16[2,64,1280]{2,1,0:T(8,128)(2,1)}, bf16[2,64,1280]{2,1,0:T(8,128)(2,1)S(1)}, u32[]{:S(2)}, u32[]{:S(2)}) %collective-permute-start.2) | collective-permute-done | bytes 327712 | tf_op jit(solution)/shard_map/ppermute | solution.py:46
  45.3 2.1 %shard_map.149 = (bf16[8,64,1280]{2,1,0:T(8,128)(2,1)S(1)}, bf16[2,64,1280]{2,1,0:T(8,128)(2,1)}, bf16[2,64,1280]{2,1,0:T(8,128)(2,1)}, bf16[2,64,1280]{2,1,0:T(8,128)(2,1)}) custom-call(s32[40]{0:T(128)S(1)} %get-tuple-element.35.table_ref, bf16[8,64,1280]{2,1,0:T(8,128)(2,1)S(1)} %copy-done.5, bf16[2,64,1280]{2,1,0:T(8,128)(2,1)} %collective-permute-done.1.rest_0_, ...), custom_call_target="tpu_custom_call" | custom-call | tf_op jit(solution)/shard_map/pallas_call | solution.py:176
  48.5 2.5 %collective-permute-start.5 = (bf16[2,64,1280]{2,1,0:T(8,128)(2,1)}, bf16[2,64,1280]{2,1,0:T(8,128)(2,1)}, u32[]{:S(2)}, u32[]{:S(2)}) collective-permute-start(bf16[2,64,1280]{2,1,0:T(8,128)(2,1)} %get-tuple-element.44), channel_id=1, source_target_pairs={{0,16},{1,17},{2,18},{3,19},{4,20},{5,21},{6,22},{7,23},{8,24},{9,... | collective-permute-start | bytes 983048 | tf_op jit(solution)/shard_map/ppermute | solution.py:46
  51.3 2.6 %collective-permute-done.13.rest_2_ = bf16[2,72,1280]{2,1,0:T(8,128)(2,1)} collective-permute-done((bf16[2,72,1280]{2,1,0:T(8,128)(2,1)}, bf16[2,72,1280]{2,1,0:T(8,128)(2,1)}, u32[]{:S(2)}, u32[]{:S(2)}) %collective-permute-start.13) | collective-permute-done | bytes 368672 | tf_op jit(solution)/shard_map/ppermute | solution.py:46
  56.3 2.5 %collective-permute-start.15 = (bf16[2,72,1280]{2,1,0:T(8,128)(2,1)S(1)}, bf16[2,72,1280]{2,1,0:T(8,128)(2,1)S(1)}, u32[]{:S(2)}, u32[]{:S(2)}) collective-permute-start(bf16[2,72,1280]{2,1,0:T(8,128)(2,1)S(1)} %get-tuple-element.58), channel_id=1, source_target_pairs={{0,16},{1,17},{2,18},{3,19},{4,20},{5,21},{6,22},{7,23},{8,24},{9,... | collective-permute-start | bytes 1105928 | tf_op jit(solution)/shard_map/ppermute | solution.py:46
  60.8 2.3 %collective-permute-done.6.rest_2_ = bf16[2,64,1280]{2,1,0:T(8,128)(2,1)} collective-permute-done((bf16[2,64,1280]{2,1,0:T(8,128)(2,1)}, bf16[2,64,1280]{2,1,0:T(8,128)(2,1)}, u32[]{:S(2)}, u32[]{:S(2)}) %collective-permute-start.6) | collective-permute-done | bytes 327712 | tf_op jit(solution)/shard_map/ppermute | solution.py:46
  63.1 2.2 %shard_map.150 = (bf16[8,64,1280]{2,1,0:T(8,128)(2,1)S(1)}, bf16[2,64,1280]{2,1,0:T(8,128)(2,1)S(1)}, bf16[2,64,1280]{2,1,0:T(8,128)(2,1)}, bf16[2,64,1280]{2,1,0:T(8,128)(2,1)}) custom-call(s32[40]{0:T(128)S(1)} %get-tuple-element.35.table_ref, bf16[8,64,1280]{2,1,0:T(8,128)(2,1)S(1)} %get-tuple-element.42.old_ref, ...), custom_call_target="tpu_custom_call" | custom-call | tf_op jit(solution)/shard_map/pallas_call | solution.py:176
  66.6 2.3 %fusion.refs_12_ = bf16[1280,1280]{1,0:T(8,128)(2,1)} fusion(s32[1280]{0:T(1024)S(1)} %eq.28), kind=kLoop, calls=%fused_computation.3 | loop fusion | flops 3276800 | bytes 3281920 | tf_op jit(solution)/shard_map/convert_element_type | solution.py:571
  68.9 2.7 %collective-permute-start.8 = (bf16[2,64,1280]{2,1,0:T(8,128)(2,1)}, bf16[2,64,1280]{2,1,0:T(8,128)(2,1)S(1)}, u32[]{:S(2)}, u32[]{:S(2)}) collective-permute-start(bf16[2,64,1280]{2,1,0:T(8,128)(2,1)} %get-tuple-element.48), channel_id=1, source_target_pairs={{0,64},{1,65},{2,66},{3,67},{4,68},{5,69},{6,70},{7,71},{8,72},{9,... | collective-permute-start | bytes 983048 | tf_op jit(solution)/shard_map/ppermute | solution.py:46
  71.7 4.8 %collective-permute-done.15.rest_1_ = bf16[2,72,1280]{2,1,0:T(8,128)(2,1)S(1)} collective-permute-done((bf16[2,72,1280]{2,1,0:T(8,128)(2,1)S(1)}, bf16[2,72,1280]{2,1,0:T(8,128)(2,1)S(1)}, u32[]{:S(2)}, u32[]{:S(2)}) %collective-permute-start.15) | collective-permute-done | bytes 368672 | tf_op jit(solution)/shard_map/ppermute | solution.py:46
  82.4 2.6 %collective-permute-start.18 = (bf16[2,72,1280]{2,1,0:T(8,128)(2,1)}, bf16[2,72,1280]{2,1,0:T(8,128)(2,1)S(1)}, u32[]{:S(2)}, u32[]{:S(2)}) collective-permute-start(bf16[2,72,1280]{2,1,0:T(8,128)(2,1)} %get-tuple-element.62), channel_id=1, source_target_pairs={{0,64},{1,65},{2,66},{3,67},{4,68},{5,69},{6,70},{7,71},{8,72},{9,... | collective-permute-start | bytes 1105928 | tf_op jit(solution)/shard_map/ppermute | solution.py:46
  85.5 2.4 %copy-done.1 = bf16[1280,1920]{1,0:T(8,128)(2,1)S(1)} copy-done((bf16[1280,1920]{1,0:T(8,128)(2,1)S(1)}, bf16[1280,1920]{1,0:T(8,128)(2,1)}, u32[]{:S(2)}) %copy-start.1) | copy-done | bytes 4915224
  89.3 2.2 %copy-done = bf16[1920,1280]{1,0:T(8,128)(2,1)} copy-done((bf16[1920,1280]{1,0:T(8,128)(2,1)}, bf16[1920,1280]{1,0:T(8,128)(2,1)S(1)}, u32[]{:S(2)}) %copy-start) | copy-done | bytes 4915224
  91.7 10.2 %collective-permute-done.18.refs_6_ = bf16[2,72,1280]{2,1,0:T(8,128)(2,1)S(1)} collective-permute-done((bf16[2,72,1280]{2,1,0:T(8,128)(2,1)}, bf16[2,72,1280]{2,1,0:T(8,128)(2,1)S(1)}, u32[]{:S(2)}, u32[]{:S(2)}) %collective-permute-start.18) | collective-permute-done | bytes 368672 | tf_op jit(solution)/shard_map/ppermute | solution.py:46
  101.9 5.6 %collective-permute-done.19.refs_7_ = bf16[2,72,1280]{2,1,0:T(8,128)(2,1)S(1)} collective-permute-done((bf16[2,72,1280]{2,1,0:T(8,128)(2,1)}, bf16[2,72,1280]{2,1,0:T(8,128)(2,1)S(1)}, u32[]{:S(2)}, u32[]{:S(2)}) %collective-permute-start.19) | collective-permute-done | bytes 368672 | tf_op jit(solution)/shard_map/ppermute | solution.py:46
  107.6 31.2 %layer.1 = (bf16[512,1280]{1,0:T(8,128)(2,1)}, bf16[64,200,128]{2,1,0:T(8,128)(2,1)}, bf16[64,200,128]{2,1,0:T(8,128)(2,1)}) custom-call(s32[40]{0:T(128)S(1)} %get-tuple-element.35.table_ref, bf16[8,64,1280]{2,1,0:T(8,128)(2,1)S(1)} %get-tuple-element.46.refs_0_, bf16[2,64,1280]{2,1,0:T(8,128)(2,1)S(1)} %collective-permute-done.7.refs_1_, ...), custom_call_target="tpu_custom_call" | custom-call | tf_op jit(solution)/shard_map/layer/pallas_call | solution.py:481
  138.7 4.4 %collective-permute-start.20 = (bf16[64,200,128]{2,1,0:T(8,128)(2,1)}, bf16[64,200,128]{2,1,0:T(8,128)(2,1)S(1)}, u32[]{:S(2)}, u32[]{:S(2)}) collective-permute-start(bf16[64,200,128]{2,1,0:T(8,128)(2,1)} %get-tuple-element.66), channel_id=1, source_target_pairs={{0,1},{1,0},{2,3},{3,2},{4,5},{5,4},{6,7},{7,6},{8,9},{9,8},{10,11... | collective-permute-start | bytes 9830408 | tf_op jit(solution)/shard_map/ppermute | solution.py:580
  143.1 5.7 %collective-permute-done.20 = bf16[64,200,128]{2,1,0:T(8,128)(2,1)S(1)} collective-permute-done((bf16[64,200,128]{2,1,0:T(8,128)(2,1)}, bf16[64,200,128]{2,1,0:T(8,128)(2,1)S(1)}, u32[]{:S(2)}, u32[]{:S(2)}) %collective-permute-start.20) | collective-permute-done | bytes 3276832 | tf_op jit(solution)/shard_map/ppermute | solution.py:580
  148.8 2.8 %add_convert_fusion = bf16[64,200,128]{2,1,0:T(8,128)(2,1)S(1)} fusion(bf16[64,200,128]{2,1,0:T(8,128)(2,1)S(1)} %collective-permute-done.20, bf16[64,200,128]{2,1,0:T(8,128)(2,1)} %get-tuple-element.65), kind=kLoop, calls=%fused_computation.1 | loop fusion | flops 6553600 | bytes 9830400 | tf_op jit(solution)/shard_map/convert_element_type | solution.py:581
  151.6 45.4 %all_to_all.5 = bf16[64,200,128]{2,1,0:T(8,128)(2,1)S(1)} all-to-all(bf16[64,200,128]{2,1,0:T(8,128)(2,1)S(1)} %add_convert_fusion), channel_id=1, replica_groups={{0,2,4,6,8,10,12,14,16,18,20,22,24,26,28,30,32,34,36,38,40,42,44,46,48,..., dimensions={0} | all-to-all | bytes 6553600 | tf_op jit(solution)/shard_map/all_to_all | solution.py:582
  (106 shorter events, 37.3 us)
Async XLA Ops:
  6.3 8.3 %collective-permute-start.10 = (bf16[2,72,1280]{2,1,0:T(8,128)(2,1)}, bf16[2,72,1280]{2,1,0:T(8,128)(2,1)S(1)}, u32[]{:S(2)}, u32[]{:S(2)}) collective-permute-start(bf16[2,72,1280]{2,1,0:T(8,128)(2,1)} %get-tuple-element.51), channel_id=1, source_target_pairs={{0,1},{1,0},{2,3},{3,2},{4,5},{5,4},{6,7},{7,6},{8,9},{9,8},{10,11... | collective-permute-start | bytes 1105928 | tf_op jit(solution)/shard_map/ppermute | solution.py:46
  7.8 2.1 %collective-permute-start = (bf16[2,64,1280]{2,1,0:T(8,128)(2,1)}, bf16[2,64,1280]{2,1,0:T(8,128)(2,1)}, u32[]{:S(2)}, u32[]{:S(2)}) collective-permute-start(bf16[2,64,1280]{2,1,0:T(8,128)(2,1)} %get-tuple-element.37), channel_id=1, source_target_pairs={{0,1},{1,0},{2,3},{3,2},{4,5},{5,4},{6,7},{7,6},{8,9},{9,8},{10,11... | collective-permute-start | bytes 983048 | tf_op jit(solution)/shard_map/ppermute | solution.py:46
  12.8 11.1 %collective-permute-start.1 = (bf16[2,64,1280]{2,1,0:T(8,128)(2,1)}, bf16[2,64,1280]{2,1,0:T(8,128)(2,1)}, u32[]{:S(2)}, u32[]{:S(2)}) collective-permute-start(bf16[2,64,1280]{2,1,0:T(8,128)(2,1)} %get-tuple-element.39), channel_id=1, source_target_pairs={{0,2},{1,3},{2,0},{3,1},{4,6},{5,7},{6,4},{7,5},{8,10},{9,11},{10,... | collective-permute-start | bytes 983048 | tf_op jit(solution)/shard_map/ppermute | solution.py:46
  17.5 33.5 %collective-permute-start.11 = (bf16[2,72,1280]{2,1,0:T(8,128)(2,1)}, bf16[2,72,1280]{2,1,0:T(8,128)(2,1)S(1)}, u32[]{:S(2)}, u32[]{:S(2)}) collective-permute-start(bf16[2,72,1280]{2,1,0:T(8,128)(2,1)} %get-tuple-element.53), channel_id=1, source_target_pairs={{0,2},{1,3},{2,0},{3,1},{4,6},{5,7},{6,4},{7,5},{8,10},{9,11},{10,... | collective-permute-start | bytes 1105928 | tf_op jit(solution)/shard_map/ppermute | solution.py:46
  17.9 22.6 %collective-permute-start.2 = (bf16[2,64,1280]{2,1,0:T(8,128)(2,1)}, bf16[2,64,1280]{2,1,0:T(8,128)(2,1)S(1)}, u32[]{:S(2)}, u32[]{:S(2)}) collective-permute-start(bf16[2,64,1280]{2,1,0:T(8,128)(2,1)} %copy-done.15), channel_id=1, source_target_pairs={{0,4},{1,5},{2,6},{3,7},{4,0},{5,1},{6,2},{7,3},{8,12},{9,13},{10,... | collective-permute-start | bytes 983048 | tf_op jit(solution)/shard_map/ppermute | solution.py:46
  21.4 19.9 %collective-permute-start.3 = (bf16[2,64,1280]{2,1,0:T(8,128)(2,1)}, bf16[2,64,1280]{2,1,0:T(8,128)(2,1)S(1)}, u32[]{:S(2)}, u32[]{:S(2)}) collective-permute-start(bf16[2,64,1280]{2,1,0:T(8,128)(2,1)} %copy-done.14), channel_id=1, source_target_pairs={{0,6},{1,7},{2,4},{3,5},{4,2},{5,3},{6,0},{7,1},{8,14},{9,15},{10,... | collective-permute-start | bytes 983048 | tf_op jit(solution)/shard_map/ppermute | solution.py:46
  21.8 29.4 %collective-permute-start.12 = (bf16[2,72,1280]{2,1,0:T(8,128)(2,1)}, bf16[2,72,1280]{2,1,0:T(8,128)(2,1)S(1)}, u32[]{:S(2)}, u32[]{:S(2)}) collective-permute-start(bf16[2,72,1280]{2,1,0:T(8,128)(2,1)} %copy-done.13), channel_id=1, source_target_pairs={{0,4},{1,5},{2,6},{3,7},{4,0},{5,1},{6,2},{7,3},{8,12},{9,13},{10,... | collective-permute-start | bytes 1105928 | tf_op jit(solution)/shard_map/ppermute | solution.py:46
  24.0 29.9 %collective-permute-start.13 = (bf16[2,72,1280]{2,1,0:T(8,128)(2,1)}, bf16[2,72,1280]{2,1,0:T(8,128)(2,1)}, u32[]{:S(2)}, u32[]{:S(2)}) collective-permute-start(bf16[2,72,1280]{2,1,0:T(8,128)(2,1)} %copy-done.12), channel_id=1, source_target_pairs={{0,6},{1,7},{2,4},{3,5},{4,2},{5,3},{6,0},{7,1},{8,14},{9,15},{10,... | collective-permute-start | bytes 1105928 | tf_op jit(solution)/shard_map/ppermute | solution.py:46
  47.4 11.5 %collective-permute-start.4 = (bf16[2,64,1280]{2,1,0:T(8,128)(2,1)}, bf16[2,64,1280]{2,1,0:T(8,128)(2,1)}, u32[]{:S(2)}, u32[]{:S(2)}) collective-permute-start(bf16[2,64,1280]{2,1,0:T(8,128)(2,1)} %get-tuple-element.43), channel_id=1, source_target_pairs={{0,8},{1,9},{2,10},{3,11},{4,12},{5,13},{6,14},{7,15},{8,0},{9,1},... | collective-permute-start | bytes 983048 | tf_op jit(solution)/shard_map/ppermute | solution.py:46
  48.5 12.3 %collective-permute-start.5 = (bf16[2,64,1280]{2,1,0:T(8,128)(2,1)}, bf16[2,64,1280]{2,1,0:T(8,128)(2,1)}, u32[]{:S(2)}, u32[]{:S(2)}) collective-permute-start(bf16[2,64,1280]{2,1,0:T(8,128)(2,1)} %get-tuple-element.44), channel_id=1, source_target_pairs={{0,16},{1,17},{2,18},{3,19},{4,20},{5,21},{6,22},{7,23},{8,24},{9,... | collective-permute-start | bytes 983048 | tf_op jit(solution)/shard_map/ppermute | solution.py:46
  51.1 12.1 %collective-permute-start.6 = (bf16[2,64,1280]{2,1,0:T(8,128)(2,1)}, bf16[2,64,1280]{2,1,0:T(8,128)(2,1)}, u32[]{:S(2)}, u32[]{:S(2)}) collective-permute-start(bf16[2,64,1280]{2,1,0:T(8,128)(2,1)} %get-tuple-element.45), channel_id=1, source_target_pairs={{0,24},{1,25},{2,26},{3,27},{4,28},{5,29},{6,30},{7,31},{8,16},{9,... | collective-permute-start | bytes 983048 | tf_op jit(solution)/shard_map/ppermute | solution.py:46
  55.1 16.6 %collective-permute-start.14 = (bf16[2,72,1280]{2,1,0:T(8,128)(2,1)S(1)}, bf16[2,72,1280]{2,1,0:T(8,128)(2,1)S(1)}, u32[]{:S(2)}, u32[]{:S(2)}) collective-permute-start(bf16[2,72,1280]{2,1,0:T(8,128)(2,1)S(1)} %get-tuple-element.57), channel_id=1, source_target_pairs={{0,8},{1,9},{2,10},{3,11},{4,12},{5,13},{6,14},{7,15},{8,0},{9,1},... | collective-permute-start | bytes 1105928 | tf_op jit(solution)/shard_map/ppermute | solution.py:46
  56.3 20.2 %collective-permute-start.15 = (bf16[2,72,1280]{2,1,0:T(8,128)(2,1)S(1)}, bf16[2,72,1280]{2,1,0:T(8,128)(2,1)S(1)}, u32[]{:S(2)}, u32[]{:S(2)}) collective-permute-start(bf16[2,72,1280]{2,1,0:T(8,128)(2,1)S(1)} %get-tuple-element.58), channel_id=1, source_target_pairs={{0,16},{1,17},{2,18},{3,19},{4,20},{5,21},{6,22},{7,23},{8,24},{9,... | collective-permute-start | bytes 1105928 | tf_op jit(solution)/shard_map/ppermute | solution.py:46
  58.9 19.5 %collective-permute-start.16 = (bf16[2,72,1280]{2,1,0:T(8,128)(2,1)S(1)}, bf16[2,72,1280]{2,1,0:T(8,128)(2,1)S(1)}, u32[]{:S(2)}, u32[]{:S(2)}) collective-permute-start(bf16[2,72,1280]{2,1,0:T(8,128)(2,1)S(1)} %get-tuple-element.59), channel_id=1, source_target_pairs={{0,24},{1,25},{2,26},{3,27},{4,28},{5,29},{6,30},{7,31},{8,16},{9,... | collective-permute-start | bytes 1105928 | tf_op jit(solution)/shard_map/ppermute | solution.py:46
  65.3 19.8 %copy-start.20 = (bf16[1280]{0:T(1024)(128)(2,1)S(1)}, bf16[1280]{0:T(1024)(128)(2,1)}, u32[]{:S(2)}) copy-start(bf16[1280]{0:T(1024)(128)(2,1)} %param.20) | copy-start | bytes 7684
  65.3 19.8 %copy-start.21 = (bf16[1280]{0:T(1024)(128)(2,1)S(1)}, bf16[1280]{0:T(1024)(128)(2,1)}, u32[]{:S(2)}) copy-start(bf16[1280]{0:T(1024)(128)(2,1)} %param.24) | copy-start | bytes 7684
  65.3 19.9 %copy-start.18 = (bf16[1920]{0:T(1024)(128)(2,1)S(1)}, bf16[1920]{0:T(1024)(128)(2,1)}, u32[]{:S(2)}) copy-start(bf16[1920]{0:T(1024)(128)(2,1)} %param.22) | copy-start | bytes 11524
  65.4 19.6 %collective-permute-start.7 = (bf16[2,64,1280]{2,1,0:T(8,128)(2,1)S(1)}, bf16[2,64,1280]{2,1,0:T(8,128)(2,1)S(1)}, u32[]{:S(2)}, u32[]{:S(2)}) collective-permute-start(bf16[2,64,1280]{2,1,0:T(8,128)(2,1)S(1)} %get-tuple-element.47), channel_id=1, source_target_pairs={{0,32},{1,33},{2,34},{3,35},{4,36},{5,37},{6,38},{7,39},{8,40},{9,... | collective-permute-start | bytes 983048 | tf_op jit(solution)/shard_map/ppermute | solution.py:46
  68.9 22.8 %collective-permute-start.8 = (bf16[2,64,1280]{2,1,0:T(8,128)(2,1)}, bf16[2,64,1280]{2,1,0:T(8,128)(2,1)S(1)}, u32[]{:S(2)}, u32[]{:S(2)}) collective-permute-start(bf16[2,64,1280]{2,1,0:T(8,128)(2,1)} %get-tuple-element.48), channel_id=1, source_target_pairs={{0,64},{1,65},{2,66},{3,67},{4,68},{5,69},{6,70},{7,71},{8,72},{9,... | collective-permute-start | bytes 983048 | tf_op jit(solution)/shard_map/ppermute | solution.py:46
  71.7 20.0 %collective-permute-start.9 = (bf16[2,64,1280]{2,1,0:T(8,128)(2,1)}, bf16[2,64,1280]{2,1,0:T(8,128)(2,1)S(1)}, u32[]{:S(2)}, u32[]{:S(2)}) collective-permute-start(bf16[2,64,1280]{2,1,0:T(8,128)(2,1)} %get-tuple-element.49), channel_id=1, source_target_pairs={{0,96},{1,97},{2,98},{3,99},{4,100},{5,101},{6,102},{7,103},{8,104... | collective-permute-start | bytes 983048 | tf_op jit(solution)/shard_map/ppermute | solution.py:46
  81.2 10.5 %collective-permute-start.17 = (bf16[2,72,1280]{2,1,0:T(8,128)(2,1)}, bf16[2,72,1280]{2,1,0:T(8,128)(2,1)S(1)}, u32[]{:S(2)}, u32[]{:S(2)}) collective-permute-start(bf16[2,72,1280]{2,1,0:T(8,128)(2,1)} %get-tuple-element.61), channel_id=1, source_target_pairs={{0,32},{1,33},{2,34},{3,35},{4,36},{5,37},{6,38},{7,39},{8,40},{9,... | collective-permute-start | bytes 1105928 | tf_op jit(solution)/shard_map/ppermute | solution.py:46
  82.4 19.6 %collective-permute-start.18 = (bf16[2,72,1280]{2,1,0:T(8,128)(2,1)}, bf16[2,72,1280]{2,1,0:T(8,128)(2,1)S(1)}, u32[]{:S(2)}, u32[]{:S(2)}) collective-permute-start(bf16[2,72,1280]{2,1,0:T(8,128)(2,1)} %get-tuple-element.62), channel_id=1, source_target_pairs={{0,64},{1,65},{2,66},{3,67},{4,68},{5,69},{6,70},{7,71},{8,72},{9,... | collective-permute-start | bytes 1105928 | tf_op jit(solution)/shard_map/ppermute | solution.py:46
  85.0 22.6 %collective-permute-start.19 = (bf16[2,72,1280]{2,1,0:T(8,128)(2,1)}, bf16[2,72,1280]{2,1,0:T(8,128)(2,1)S(1)}, u32[]{:S(2)}, u32[]{:S(2)}) collective-permute-start(bf16[2,72,1280]{2,1,0:T(8,128)(2,1)} %get-tuple-element.63), channel_id=1, source_target_pairs={{0,96},{1,97},{2,98},{3,99},{4,100},{5,101},{6,102},{7,103},{8,104... | collective-permute-start | bytes 1105928 | tf_op jit(solution)/shard_map/ppermute | solution.py:46
  138.7 10.1 %collective-permute-start.20 = (bf16[64,200,128]{2,1,0:T(8,128)(2,1)}, bf16[64,200,128]{2,1,0:T(8,128)(2,1)S(1)}, u32[]{:S(2)}, u32[]{:S(2)}) collective-permute-start(bf16[64,200,128]{2,1,0:T(8,128)(2,1)} %get-tuple-element.66), channel_id=1, source_target_pairs={{0,1},{1,0},{2,3},{3,2},{4,5},{5,4},{6,7},{7,6},{8,9},{9,8},{10,11... | collective-permute-start | bytes 9830408 | tf_op jit(solution)/shard_map/ppermute | solution.py:580
  (19 other events, 71.3 us)
